TPU v7x, 512 devices: a whole 4x8x8 slice. The times are simulated.
512 devices in a mesh: dp: 8 (over x, core), expert: 64 (over y, z).
Axes of the slice: x: 4, y: 8, z: 8, core: 2. Of those that a mesh axis runs over, the one named last changes fastest.
Arguments:
- grad_out: bfloat16 [65536, 2048], P(('dp', 'expert')), may hold values from -6 to 6
- expert_ids: int32 [65536, 6], P(('dp', 'expert')), may hold values from 0 to 63, all different within a row; in each aligned block of 128 rows (0 to 127, 128 to 255, ...) at most 16 rows name the same one
- gates: bfloat16 [65536, 6], P(('dp', 'expert')), may hold values from 0.049804688 to 1
- hidden: bfloat16 [524288, 704], P(('dp', 'expert')), may hold values from -6 to 6
- w_down: bfloat16 [64, 2048, 704], P('expert', 'dp'), may hold values from -0.21875 to 0.21875
Outputs:
- grad_hidden: bfloat16 [524288, 704], P(('dp', 'expert'))
- grad_down: float32 [64, 2048, 704], P('expert', 'dp')
- grad_gates: float32 [65536, 6], P(('dp', 'expert'))
Inputs may be any that keep to these rules, and one draw needn't show every extreme that they name: `expert_ids`: in the rows of one device no expert is named by more than 16 rows; in every draw some device has an expert named by exactly 16 of its rows. A row names 6 different experts.
All inputs are finite; a program needn't handle non-finite values.
Results may differ from a plain program's by a relative error of at most 0.012.
Values may be sent and summed in bfloat16 or wider, within the bound.
No kernel may reach another device: no remote copies, remote signals or barrier semaphores. Data moves between devices by JAX's collectives and lax.ppermute only.
A program may use at most 64 MiB of HBM per device.

v0:
```python
import jax
import jax.numpy as jnp
from jax import lax
from jax.sharding import PartitionSpec as P


def shards(grad_out, expert_ids, gates, hidden, w_down):
    experts = lax.axis_size("expert")
    tok_rows = grad_out.shape[0]
    width = grad_out.shape[1]
    top_count = expert_ids.shape[1]
    slot_rows = hidden.shape[0]
    per_source = slot_rows // experts
    ids_flat = expert_ids.reshape(-1)
    onehot = (ids_flat[:, None] == jnp.arange(experts, dtype=jnp.int32)[None, :]).astype(jnp.int32)
    before = jnp.cumsum(onehot, axis=0) - onehot
    ranks = jnp.sum(before * onehot, axis=1)
    target = (ids_flat * per_source + ranks).reshape(tok_rows, top_count)
    slot_index = jnp.arange(slot_rows, dtype=jnp.int32)
    match = target[None, :, :] == slot_index[:, None, None]
    select = jnp.any(match, axis=2).astype(jnp.bfloat16)
    gate_pick = jnp.sum(jnp.where(match, gates.astype(jnp.float32)[None, :, :], 0.0), axis=(1, 2))
    send_rows = jnp.dot(select, grad_out, preferred_element_type=jnp.float32).astype(jnp.bfloat16)
    send_gate = gate_pick.astype(jnp.bfloat16)
    recv_rows, recv_gate = (
        lax.all_to_all(
            send_rows.reshape(experts, per_source, width),
            "expert",
            split_axis=0,
            concat_axis=0,
            tiled=True,
        ),
        lax.all_to_all(
            send_gate.reshape(experts, per_source),
            "expert",
            split_axis=0,
            concat_axis=0,
            tiled=True,
        ),
    )
    dispatched = recv_rows.reshape(slot_rows, width)
    gate_row = recv_gate.reshape(slot_rows).astype(jnp.float32)
    u_rows = jnp.dot(
        dispatched,
        lax.all_gather(w_down, "dp", axis=1, tiled=True)[0],
        preferred_element_type=jnp.float32,
    )
    grad_hidden = (gate_row[:, None] * u_rows).astype(jnp.bfloat16)
    scaled = (gate_row[:, None] * dispatched.astype(jnp.float32)).astype(jnp.bfloat16)
    partial_grad = lax.dot_general(
        scaled, hidden, (((0,), (0,)), ((), ())), preferred_element_type=jnp.float32
    )
    grad_down = lax.psum_scatter(
        partial_grad.astype(jnp.bfloat16), "dp", scatter_dimension=0, tiled=True
    ).astype(jnp.float32)
    slot_grad = jnp.sum(hidden.astype(jnp.float32) * u_rows, axis=1)
    returned = lax.all_to_all(
        slot_grad.reshape(experts, per_source), "expert", split_axis=0, concat_axis=0, tiled=True
    )
    grad_gates = jnp.take(returned.reshape(-1), target.reshape(-1)).reshape(tok_rows, top_count)
    return (grad_hidden, grad_down.reshape(1, grad_down.shape[0], grad_down.shape[1]), grad_gates)


def solution(mesh):
    return jax.shard_map(
        shards,
        mesh=mesh,
        in_specs=(
            P(("dp", "expert"), None),
            P(("dp", "expert"), None),
            P(("dp", "expert"), None),
            P(("dp", "expert"), None),
            P("expert", "dp", None),
        ),
        out_specs=(P(("dp", "expert"), None), P("expert", "dp", None), P(("dp", "expert"), None)),
        check_vma=False,
    )
```

profile of v0, /device:TPU:8, one launch (start us, length us, event | category | flops | bytes accessed | tf_op | source)
XLA Modules:
  0.0 230.8 jit_solution(11221788013342170481)
XLA Ops:
  7.2 0.0 copy-start
  7.2 0.9 copy.24
  8.0 0.1 eq.42
  8.2 0.1 eq.38
  8.3 1.8 reduce-window.6
  10.1 0.3 slice_reduce_fusion
  10.4 0.1 fusion.8
  10.6 0.1 reduce_sum.32
  10.7 0.1 copy.28
  10.8 0.7 convert_element_type.56
  11.5 0.4 select_reduce_fusion
  11.9 0.7 convert_element_type.68
  12.6 16.6 %all-to-all-start = ((bf16[64,1,16]{2,1,0:T(2,128)(2,1)}), bf16[64,1,16]{2,1,0:T(2,128)(2,1)S(1)}, u32[]{:S(2)}, u32[]{:S(2)}) async-start(bf16[64,1,16]{2,1,0:T(2,128)(2,1)} %convert_element_type.68), calls=%async_computation | async-start | bytes 65536 | tf_op jit(solution)/shard_map/all_to_all | solution.py:33
  29.2 0.5 fusion.3
  29.7 0.0 copy-done
  29.7 3.2 %convolution_convert_fusion = bf16[1024,2048]{1,0:T(8,128)(2,1)} fusion(pred[1024,128]{1,0:T(8,128)(4,1)S(1)} %fusion.3, bf16[128,2048]{1,0:T(8,128)(2,1)S(1)} %copy-done), kind=kOutput, calls=%fused_computation.4 | convolution fusion | flops 538968064 | bytes 4849664 | tf_op jit(solution)/shard_map/dot_general | solution.py:23
  32.9 7.3 %all-to-all-done = bf16[64,1,16]{2,1,0:T(2,128)(2,1)S(1)} async-done(((bf16[64,1,16]{2,1,0:T(2,128)(2,1)}), bf16[64,1,16]{2,1,0:T(2,128)(2,1)S(1)}, u32[]{:S(2)}, u32[]{:S(2)}) %all-to-all-start) | async-done | bytes 2080 | tf_op jit(solution)/shard_map/all_to_all | solution.py:33
  40.2 0.0 copy-start.1
  40.2 6.6 %all-to-all-start.1 = ((bf16[64,16,2048]{2,1,0:T(8,128)(2,1)}), bf16[64,16,2048]{2,1,0:T(8,128)(2,1)}, u32[]{:S(2)}, u32[]{:S(2)}) async-start(bf16[64,16,2048]{2,1,0:T(8,128)(2,1)} %bitcast.35), calls=%async_computation.1 | async-start | bytes 8388608 | tf_op jit(solution)/shard_map/all_to_all | solution.py:26
  46.8 0.0 all-gather.2.cloned.1.call-start
  46.8 0.7 all-gather.2.cloned.1.call-update
  47.5 0.0 reduce-scatter.2.cloned.1.call-start
  47.6 0.1 convert_reduce_fusion
  47.7 0.1 reshape.119
  47.7 111.2 %all-to-all-done.1 = bf16[64,16,2048]{2,1,0:T(8,128)(2,1)} async-done(((bf16[64,16,2048]{2,1,0:T(8,128)(2,1)}), bf16[64,16,2048]{2,1,0:T(8,128)(2,1)}, u32[]{:S(2)}, u32[]{:S(2)}) %all-to-all-start.1) | async-done | bytes 4194336 | tf_op jit(solution)/shard_map/all_to_all | solution.py:26
  158.9 0.0 copy-done.1
  158.9 6.9 %fusion.2 = bf16[2048,704]{0,1:T(8,128)(2,1)} fusion(bf16[1024,704]{0,1:T(8,128)(2,1)S(1)} %copy-done.1, bf16[1024,2048]{1,0:T(8,128)(2,1)} %bitcast.2, f32[1024]{0:T(1024)S(1)} %reshape.119), kind=kOutput, calls=%fused_computation.5 | convolution fusion | flops 2960523264 | bytes 8523776 | tf_op jit(solution)/shard_map/dot_general | solution.py:50
  165.8 0.0 reduce-scatter.2.cloned.1.call-update
  165.9 0.1 mul.51
  166.0 0.0 all-gather.2.cloned.1.call-done
  166.1 7.4 %multiply_reduce_fusion = (f32[1024]{0:T(1024)S(1)}, bf16[1024,704]{0,1:T(8,128)(2,1)}) fusion(bf16[1024,704]{0,1:T(8,128)(2,1)S(1)} %copy-done.1, f32[1024]{0:T(1024)S(1)} %reshape.119, bf16[1024,2048]{1,0:T(8,128)(2,1)} %bitcast.2, bf16[1,2048,704]{1,2,0:T(8,128)(2,1)} %all-gather.2.cloned.1.call-done), kind=kOutput, calls=%fused_computation.11 | convolution fusion | flops 2956393472 | bytes 9969664 | tf_op jit(solution)/shard_map/dot_general | solution.py:43
  173.5 0.7 all_to_all.15
  174.2 27.0 %all-to-all-start.2 = ((f32[64,1,16]{2,1,0:T(1,128)}), f32[64,1,16]{2,1,0:T(1,128)S(1)}, u32[]{:S(2)}, u32[]{:S(2)}) async-start(f32[64,1,16]{2,1,0:T(1,128)} %bitcast.5), calls=%async_computation.3 | async-start | bytes 65536 | tf_op jit(solution)/shard_map/all_to_all | solution.py:57
  201.2 11.0 %all-to-all-done.2 = f32[64,1,16]{2,1,0:T(1,128)S(1)} async-done(((f32[64,1,16]{2,1,0:T(1,128)}), f32[64,1,16]{2,1,0:T(1,128)S(1)}, u32[]{:S(2)}, u32[]{:S(2)}) %all-to-all-start.2) | async-done | bytes 4128 | tf_op jit(solution)/shard_map/all_to_all | solution.py:57
  212.2 0.5 broadcast.75
  212.7 0.7 reduce.11
  213.4 0.1 reshape.118
  213.5 3.2 %gather_fusion = f32[768]{0:T(1024)S(1)} fusion(f32[1024]{0:T(1024)S(1)} %reshape.118, s32[1024]{0:T(1024)S(1)} %pad_clamp_fusion), kind=kCustom, calls=%fused_computation | custom fusion | bytes 9216 | tf_op jit(solution)/shard_map/jit(_take)/gather | solution.py:60
  216.7 0.1 gather.7
  216.9 0.7 copy.31
  217.5 4.5 %reduce-scatter.2.cloned.1.call-done = bf16[256,704]{0,1:T(8,128)(2,1)} async-done(((bf16[2048,704]{0,1:T(8,128)(2,1)}), bf16[256,704]{0,1:T(8,128)(2,1)}) %reduce-scatter.2.cloned.1.call-update) | async-done | bytes 360464 | tf_op jit(solution)/shard_map/reduce_scatter | solution.py:53
  222.0 1.9 bitcast_convert_fusion
  (6 shorter events, 0.1 us)
Async XLA Ops:
  7.2 22.5 %copy-start = (bf16[128,2048]{1,0:T(8,128)(2,1)S(1)}, bf16[128,2048]{1,0:T(8,128)(2,1)}, u32[]{:S(2)}) copy-start(bf16[128,2048]{1,0:T(8,128)(2,1)} %param.5) | copy-start | bytes 1572868
  12.6 27.6 %all-to-all-start = ((bf16[64,1,16]{2,1,0:T(2,128)(2,1)}), bf16[64,1,16]{2,1,0:T(2,128)(2,1)S(1)}, u32[]{:S(2)}, u32[]{:S(2)}) async-start(bf16[64,1,16]{2,1,0:T(2,128)(2,1)} %convert_element_type.68), calls=%async_computation | async-start | bytes 65536 | tf_op jit(solution)/shard_map/all_to_all | solution.py:33
  40.2 118.8 %copy-start.1 = (bf16[1024,704]{0,1:T(8,128)(2,1)S(1)}, bf16[1024,704]{0,1:T(8,128)(2,1)}, u32[]{:S(2)}) copy-start(bf16[1024,704]{0,1:T(8,128)(2,1)} %param.8) | copy-start | bytes 4325380
  40.2 118.8 %all-to-all-start.1 = ((bf16[64,16,2048]{2,1,0:T(8,128)(2,1)}), bf16[64,16,2048]{2,1,0:T(8,128)(2,1)}, u32[]{:S(2)}, u32[]{:S(2)}) async-start(bf16[64,16,2048]{2,1,0:T(8,128)(2,1)} %bitcast.35), calls=%async_computation.1 | async-start | bytes 8388608 | tf_op jit(solution)/shard_map/all_to_all | solution.py:26
  46.8 119.3 %all-gather.2.cloned.1.call-start = ((), (), s32[]{:S(2)}) async-start(), calls=%async_computation.4 | async-start | bytes 3244032 | tf_op jit(solution)/shard_map/all_gather | solution.py:45
  47.5 174.5 %reduce-scatter.2.cloned.1.call-start = ((), (), s32[]{:S(2)}) async-start(), calls=%async_computation.5 | async-start | bytes 3244032 | tf_op jit(solution)/shard_map/reduce_scatter | solution.py:53
  174.2 38.0 %all-to-all-start.2 = ((f32[64,1,16]{2,1,0:T(1,128)}), f32[64,1,16]{2,1,0:T(1,128)S(1)}, u32[]{:S(2)}, u32[]{:S(2)}) async-start(f32[64,1,16]{2,1,0:T(1,128)} %bitcast.5), calls=%async_computation.3 | async-start | bytes 65536 | tf_op jit(solution)/shard_map/all_to_all | solution.py:57
Sparse Core Ops, SparseCore 0:
  49.7 36.0 all-gather.1
  166.0 56.0 reduce-scatter.1
where the time goes:
time: 231 us
  waiting for transfers between devices  135 us (58%)
  starting transfers between devices  50.3 us (22%)
  matrix products  17.5 us (8%)
  between operations  14.2 us (6%)
  local copies, waits for them, and re-layouts  7.77 us (3%)
  other arithmetic  6.35 us (3%)
    all_to_all x1, waiting for transfers between devices, shards(): lax.all_to_all(send_rows.reshape(experts, per_source, width), 'expert', s...  111 us
    all_to_all x1, starting transfers between devices, shards(): lax.all_to_all(slot_grad.reshape(experts, per_source), 'expert', split_ax...  27 us
    all_to_all x1, starting transfers between devices, shards(): lax.all_to_all(send_gate.reshape(experts, per_source), 'expert', split_ax...  16.6 us
    all_to_all x1, waiting for transfers between devices, shards(): lax.all_to_all(slot_grad.reshape(experts, per_source), 'expert', split_ax...  11 us
    dot_general x1, matrix products, shards(): jnp.dot(dispatched, lax.all_gather(w_down, 'dp', axis=1, tiled=True)[0],...  7.44 us
    all_to_all x1, waiting for transfers between devices, shards(): lax.all_to_all(send_gate.reshape(experts, per_source), 'expert', split_ax...  7.25 us
    dot_general x1, matrix products, shards(): lax.dot_general(scaled, hidden, (((0,), (0,)), ((), ())), preferred_eleme...  6.89 us
    all_to_all x1, starting transfers between devices, shards(): lax.all_to_all(send_rows.reshape(experts, per_source, width), 'expert', s...  6.6 us
  transfers between devices with their start and end apart: 5, of which 4 were waited for; matrix products, arithmetic and copies ran while one was open for 10% of the time, Pallas kernels for 0%

commit v1 on v0

v1 whole, which is shorter than its diff:
```python
import jax
import jax.numpy as jnp
from jax import lax
from jax.experimental import pallas as pl
from jax.experimental.pallas import tpu as pltpu
from jax.sharding import PartitionSpec as P


SIDE = 8
CAP = 16
LINE = SIDE * CAP
CHIPS = 4
LANES = 128
TOP = 6
OFFSETS = [0, -1, 1, -2, 2, -3, 3, -4]
EARLY, LATE = [0, 4, 1, 7, 3, 2], [6, 5]
VMEM = pl.BlockSpec(memory_space=pltpu.VMEM)
SMEM = pl.BlockSpec(memory_space=pltpu.SMEM)


def move_x(a, k):
    return lax.ppermute(a, "dp", [(x * 2 + c, (x + k) % CHIPS * 2 + c) for x in range(CHIPS) for c in range(2)])


def swap_core(a):
    return lax.ppermute(a, "dp", [(x * 2 + c, x * 2 + 1 - c) for x in range(CHIPS) for c in range(2)])


def move_plane(a, k, first_axis):
    pairs = []
    for dp in range(2 * CHIPS):
        for y in range(SIDE):
            for z in range(SIDE):
                to = ((y + k) % SIDE, z) if dp % 2 == first_axis else (y, (z + k) % SIDE)
                pairs.append(((dp * SIDE + y) * SIDE + z, (dp * SIDE + to[0]) * SIDE + to[1]))
    return lax.ppermute(a, ("dp", "expert"), pairs)


def exchange(a):
    return lax.all_to_all(a, "expert", split_axis=0, concat_axis=0, tiled=True)


def head_kernel(place_ref, ids_ref, gates_ref, tokens_ref, own_ref, other_ref, target_ref):
    tokens, share = tokens_ref.shape[0], tokens_ref.shape[1] // (2 * CHIPS)
    experts = SIDE * SIDE
    row = lax.broadcasted_iota(jnp.int32, (tokens, tokens), 0)
    earlier = (row < lax.broadcasted_iota(jnp.int32, (tokens, tokens), 1)).astype(jnp.bfloat16)
    expert = lax.broadcasted_iota(jnp.int32, (experts, tokens), 0)
    hot = [(expert == ids_ref[k : k + 1, :]).astype(jnp.float32) for k in range(TOP)]
    before = jnp.dot(sum(hot).astype(jnp.bfloat16), earlier, preferred_element_type=jnp.float32)
    ranks = [jnp.sum(h * before, axis=0, keepdims=True) for h in hot]
    blank = jnp.zeros((2, tokens), jnp.float32)
    ids = jnp.concatenate([ids_ref[...].astype(jnp.float32), blank - 1.0], axis=0)
    ranks = jnp.concatenate(ranks + [blank], axis=0)
    gates = jnp.concatenate([gates_ref[...].astype(jnp.float32), blank], axis=0)
    target_ref[...] = (ids * CAP + ranks).astype(jnp.int32)
    for half, out_ref in enumerate((own_ref, other_ref)):
        for b in range(CHIPS):
            start = pl.multiple_of(place_ref[half * CHIPS + b] * share, share)
            out_ref[0:tokens, b * share : (b + 1) * share] = tokens_ref[:, pl.ds(start, share)]
        for n, part in enumerate((ids, ranks, gates)):
            out_ref[tokens : tokens + 8, n * tokens : (n + 1) * tokens] = part.astype(jnp.bfloat16)
        out_ref[tokens : tokens + 8, 3 * tokens :] = jnp.zeros(
            (8, out_ref.shape[1] - 3 * tokens), jnp.bfloat16
        )


def route_kernel(place_ref, want_ref, *refs):
    blocks, outs = refs[:SIDE], refs[SIDE:]
    want = want_ref[...]
    ones = jnp.ones((LINE, LANES), jnp.bfloat16)
    for d in range(SIDE):
        place = place_ref[d]
        for i in range(2):
            meta = blocks[d][i, LINE : LINE + 8, 0 : 3 * LINE].astype(jnp.float32)
            target = meta[:, 0:LINE] * CAP + meta[:, LINE : 2 * LINE]
            gates = meta[:, 2 * LINE : 3 * LINE]
            select = jnp.zeros((LINE, LINE), jnp.float32)
            weigh = jnp.zeros((LINE, LINE), jnp.float32)
            for k in range(TOP):
                hit = target[k : k + 1, :] == want
                select = jnp.where(hit, 1.0, select)
                if i == 0:
                    weigh = jnp.where(hit, gates[k : k + 1, :], weigh)
            rows = jnp.dot(
                select.astype(jnp.bfloat16), blocks[d][i, 0:LINE, :], preferred_element_type=jnp.float32
            ).astype(jnp.bfloat16)
            start = pl.multiple_of(i * LINE + place * CAP, CAP)
            for k in range(SIDE):
                outs[k][pl.ds(start, CAP), :] = rows[k * CAP : (k + 1) * CAP, :]
            if i == 0:
                wide = jnp.dot(weigh.astype(jnp.bfloat16), ones, preferred_element_type=jnp.float32)
                wide = wide.astype(jnp.bfloat16)
                lane = pl.multiple_of(place * LANES, LANES)
                for k in range(SIDE):
                    outs[k][2 * LINE :, pl.ds(lane, LANES)] = wide[k * CAP : (k + 1) * CAP, :]


def join_kernel(slots_ref, *refs):
    kept, early_ref, late_ref = refs[:SIDE], refs[SIDE], refs[SIDE + 1]
    rows_ref, scaled_ref, gate_ref = refs[SIDE + 2 :]
    half = rows_ref.shape[1] // 2
    for k in range(SIDE):
        for j in range(SIDE):
            slot = pl.ds(pl.multiple_of(slots_ref[0, k * SIDE + j] * CAP, CAP), CAP)
            gate = kept[k][2 * LINE :, j * LANES : (j + 1) * LANES]
            rows = kept[k][j * CAP : (j + 1) * CAP, :]
            gate_ref[slot, :] = gate
            rows_ref[slot, 0:half] = rows
            scaled_ref[slot, 0:half] = rows * jnp.concatenate([gate] * (half // LANES), axis=1)
    for ref, order in ((early_ref, EARLY), (late_ref, LATE)):
        for n, k in enumerate(order):
            for j in range(SIDE):
                slot = pl.ds(pl.multiple_of(slots_ref[1, k * SIDE + j] * CAP, CAP), CAP)
                rows = ref[n, j * CAP : (j + 1) * CAP, :]
                rows_ref[slot, half:] = rows
                scaled_ref[slot, half:] = rows * jnp.concatenate([gate_ref[slot, :]] * (half // LANES), axis=1)


def pick_kernel(target_ref, table_ref, out_ref):
    experts, caps = table_ref.shape
    rest, pieces = table_ref[...], []
    for _ in range(3):
        piece = rest.astype(jnp.bfloat16)
        pieces.append(piece)
        rest = rest - piece.astype(jnp.float32)
    tokens = out_ref.shape[1]
    expert = lax.broadcasted_iota(jnp.int32, (experts, tokens), 0)
    cap = lax.broadcasted_iota(jnp.int32, (caps, tokens), 0)
    for k in range(out_ref.shape[0]):
        target = target_ref[k : k + 1, :]
        hot = (expert == target // caps).astype(jnp.bfloat16)
        found = sum(
            lax.dot_general(p, hot, (((0,), (0,)), ((), ())), preferred_element_type=jnp.float32) for p in pieces
        )
        out_ref[k : k + 1, :] = jnp.sum(jnp.where(cap == target % caps, found, 0.0), axis=0, keepdims=True)


def pick(target, table):
    return pl.pallas_call(
        pick_kernel,
        out_shape=jax.ShapeDtypeStruct(target.shape, jnp.float32),
        in_specs=[pl.BlockSpec(memory_space=pltpu.VMEM)] * 2,
        out_specs=pl.BlockSpec(memory_space=pltpu.VMEM),
        name="pick",
    )(target, table)


def shards(grad_out, expert_ids, gates, hidden, w_down):
    bf16, f32, i32 = jnp.bfloat16, jnp.float32, jnp.int32
    experts = lax.axis_size("expert")
    tok_rows, width = grad_out.shape
    slot_rows, units = hidden.shape
    half = width // 2
    me, dp = lax.axis_index("expert"), lax.axis_index("dp")
    my_y, my_z, my_x, my_c = me // SIDE, me % SIDE, dp // 2, dp % 2
    along = jnp.where(my_c == 0, my_y, my_z)
    across = jnp.where(my_c == 0, my_z, my_y)

    b = jnp.arange(2 * CHIPS, dtype=i32)
    place = (my_x + b % CHIPS) % CHIPS * 2 + (my_c + b // CHIPS) % 2
    block = jax.ShapeDtypeStruct((tok_rows + 8, half), bf16)
    own, other, target = pl.pallas_call(
        head_kernel,
        out_shape=(block, block, jax.ShapeDtypeStruct((8, tok_rows), i32)),
        in_specs=[SMEM, VMEM, VMEM, VMEM],
        out_specs=(VMEM,) * 3,
        name="head",
    )(place, expert_ids.T, gates.T, grad_out)

    lent = swap_core(other)
    pair = jnp.stack([own, lent])
    minus_2, plus_2 = move_plane(pair, 2, 0), move_plane(pair, -2, 0)
    minus_1, plus_1 = move_plane(pair, 1, 0), move_plane(pair, -1, 0)
    minus_4 = move_plane(minus_2, 2, 0)
    minus_3, plus_3 = move_plane(minus_2, 1, 0), move_plane(plus_2, -1, 0)
    found = [pair, minus_1, plus_1, minus_2, plus_2, minus_3, plus_3, minus_4]

    slot = jnp.arange(LINE, dtype=i32)
    step, cap = (across + slot // CAP) % SIDE, slot % CAP
    want = jnp.where(my_c == 0, my_y * SIDE + step, step * SIDE + my_z) * CAP + cap
    routed = pl.pallas_call(
        route_kernel,
        out_shape=(jax.ShapeDtypeStruct((2 * LINE + CAP, half), bf16),) * SIDE,
        in_specs=[SMEM] + [VMEM] * (SIDE + 1),
        out_specs=(VMEM,) * SIDE,
        name="route",
    )((along + jnp.array(OFFSETS, i32)) % SIDE, jnp.broadcast_to(want.astype(f32)[:, None], (LINE, tok_rows)), *found)
    kept = list(routed)
    for k in [4, 3, 5, 2, 6, 1, 7]:
        kept[k] = move_plane(routed[k], k, 1)
    early = swap_core(jnp.stack([kept[k][LINE : 2 * LINE] for k in EARLY]))
    late = swap_core(jnp.stack([kept[k][LINE : 2 * LINE] for k in LATE]))
    k, j = jnp.arange(SIDE, dtype=i32)[:, None], jnp.arange(SIDE, dtype=i32)[None, :]
    by_z, by_y = j * SIDE + (my_z - k) % SIDE, (my_y - k) % SIDE * SIDE + j
    slots = jnp.stack([jnp.where(my_c == 0, by_z, by_y).reshape(-1), jnp.where(my_c == 0, by_y, by_z).reshape(-1)])
    full = jax.ShapeDtypeStruct((slot_rows, width), bf16)
    rows, scaled, gate_wide = pl.pallas_call(
        join_kernel,
        out_shape=(full, full, jax.ShapeDtypeStruct((slot_rows, LANES), bf16)),
        in_specs=[SMEM] + [VMEM] * (SIDE + 2),
        out_specs=(VMEM,) * 3,
        name="join",
    )(slots, *kept, early, late)
    gate_row = gate_wide[:, :1].astype(f32)

    own_w = w_down[0]
    moved = [move_x(own_w, -k) for k in range(1, CHIPS)]
    same_core = jnp.stack([own_w] + moved)
    other_core = swap_core(same_core)
    weight = jnp.concatenate([same_core, other_core]).reshape(width, units)

    def share_of(columns):
        product = lax.dot_general(columns, hidden, (((0,), (0,)), ((), ())), preferred_element_type=f32)
        return product.astype(bf16).reshape((CHIPS,) + own_w.shape)

    give = share_of(scaled[:, width // 2 :])
    other = swap_core(give)
    both = share_of(scaled[:, : width // 2]).astype(f32) + other.astype(f32)
    grad_down = both[0]
    for k in (2, 1, 3):
        moved = move_x(both[k].astype(bf16), k)
        grad_down = grad_down + moved.astype(f32)

    u_rows = jnp.dot(rows, weight, preferred_element_type=f32)
    grad_hidden = (gate_row * u_rows).astype(bf16)
    slot_grad = jnp.sum(hidden.astype(f32) * u_rows, axis=1)

    returned = exchange(slot_grad.reshape(experts, CAP))
    grad_gates = pick(target, returned)[:TOP].T
    return (grad_hidden, grad_down[None], grad_gates)


def solution(mesh):
    return jax.shard_map(
        shards,
        mesh=mesh,
        in_specs=(
            P(("dp", "expert"), None),
            P(("dp", "expert"), None),
            P(("dp", "expert"), None),
            P(("dp", "expert"), None),
            P("expert", "dp", None),
        ),
        out_specs=(P(("dp", "expert"), None), P("expert", "dp", None), P(("dp", "expert"), None)),
        check_vma=False,
    )
```

time: 231 us -> 222 us (0.961)
  waiting for transfers between devices: 135 us -> 49.2 us
  starting transfers between devices: 50.3 us -> 97.1 us
  blocking collectives: 0 us -> 26.1 us
  Pallas kernels: 0 us -> 16.1 us
  between operations: 14.2 us -> 1.31 us
  matrix products: 17.5 us -> 9.78 us
  local copies, waits for them, and re-layouts: 7.77 us -> 13.1 us
    all_to_all x3 -> x0, waiting for transfers between devices: 129 us -> none  [the longest x1 111 us: shards(): lax.all_to_all(send_rows.reshape(experts, per_source, width), 'expert', s...]
    ppermute x0 -> x25, starting transfers between devices: none -> 97.1 us  [the longest x14 65.2 us: move_plane(): return lax.ppermute(a, ('dp', 'expert'), pairs)]
    all_to_all x3 -> x0, starting transfers between devices: 50.2 us -> none  [the longest x1 27 us: shards(): lax.all_to_all(slot_grad.reshape(experts, per_source), 'expert', split_ax...]
    ppermute x0 -> x25, waiting for transfers between devices: none -> 49.2 us  [the longest x14 40.3 us: move_plane(): return lax.ppermute(a, ('dp', 'expert'), pairs)]
    all_to_all x0 -> x1, blocking collectives: none -> 26.1 us  [exchange(): return lax.all_to_all(a, 'expert', split_axis=0, concat_axis=0, tiled=True)]
    pallas_call x0 -> x4, Pallas kernels: none -> 16.1 us  [the longest x1 6.8 us: shards(): pl.pallas_call(join_kernel, out_shape=(full, full, jax.ShapeDtypeStruct((...]
    dot_general x3, matrix products: 17.5 us -> 9.78 us  [the longest x2 5.37 us: share_of(): lax.dot_general(columns, hidden, (((0,), (0,)), ((), ())), preferred_elem...]
    unnamed x6 -> x61, local copies, waits for them, and re-layouts: 1.53 us -> 7.14 us
  transfers between devices with their start and end apart: 5 -> 25, of which waited for: 4 -> 11; matrix products, arithmetic and copies ran while one was open for 10% -> 10% of each run, Pallas kernels for 0% -> 4%
where the time goes in v1:
time: 222 us; the launch traced here: 221 us
  starting transfers between devices  97.1 us (44%)
  waiting for transfers between devices  49.2 us (22%)
  blocking collectives  26.1 us (12%)
  Pallas kernels  16.1 us (7%)
  local copies, waits for them, and re-layouts  13.1 us (6%)
  matrix products  9.78 us (4%)
  other arithmetic  7.78 us (4%)
    ppermute x14, starting transfers between devices, move_plane(): return lax.ppermute(a, ('dp', 'expert'), pairs)  65.2 us
    ppermute x14, waiting for transfers between devices, move_plane(): return lax.ppermute(a, ('dp', 'expert'), pairs)  40.3 us
    all_to_all x1, blocking collectives, exchange(): return lax.all_to_all(a, 'expert', split_axis=0, concat_axis=0, tiled=True)  26.1 us
    ppermute x6, starting transfers between devices, move_x(): lax.ppermute(a, 'dp', [(x * 2 + c, (x + k) % CHIPS * 2 + c) for x in rang...  20.1 us
    ppermute x5, starting transfers between devices, swap_core(): lax.ppermute(a, 'dp', [(x * 2 + c, x * 2 + 1 - c) for x in range(CHIPS) f...  11.8 us
    ppermute x6, waiting for transfers between devices, move_x(): lax.ppermute(a, 'dp', [(x * 2 + c, (x + k) % CHIPS * 2 + c) for x in rang...  7.2 us
    unnamed x61, local copies, waits for them, and re-layouts  7.14 us
    pallas_call x1, Pallas kernels, shards(): pl.pallas_call(join_kernel, out_shape=(full, full, jax.ShapeDtypeStruct((...  6.8 us
  transfers between devices with their start and end apart: 25, of which 11 were waited for; matrix products, arithmetic and copies ran while one was open for 10% of the time, Pallas kernels for 4%

profile of v1, /device:TPU:8, one launch (start us, length us, event | category | flops | bytes accessed | tf_op | source)
XLA Modules:
  0.0 220.5 jit_solution(5756222890661736186)
XLA Ops:
  1.2 2.0 head.1
  3.2 1.9 collective-permute-start
  5.1 1.7 collective-permute-done
  7.9 4.5 %collective-permute-start.3 = (bf16[2,136,1024]{2,1,0:T(8,128)(2,1)S(1)}, bf16[2,136,1024]{2,1,0:T(8,128)(2,1)S(1)}, u32[]{:S(2)}, u32[]{:S(2)}) collective-permute-start(bf16[2,136,1024]{2,1,0:T(8,128)(2,1)S(1)} %pad_maximum_fusion.1.refs_0_), channel_id=1, source_target_pairs={{0,16},{1,17},{2,18},{3,19},{4,20},{5,21},{6,22},{7,23},{8,24},{9,... | collective-permute-start | bytes 1671176 | tf_op jit(solution)/shard_map/ppermute | solution.py:36
  12.4 3.5 %collective-permute-start.4 = (bf16[2,136,1024]{2,1,0:T(8,128)(2,1)S(1)}, bf16[2,136,1024]{2,1,0:T(8,128)(2,1)S(1)}, u32[]{:S(2)}, u32[]{:S(2)}) collective-permute-start(bf16[2,136,1024]{2,1,0:T(8,128)(2,1)S(1)} %pad_maximum_fusion.1.refs_0_), channel_id=1, source_target_pairs={{0,48},{1,49},{2,50},{3,51},{4,52},{5,53},{6,54},{7,55},{8,56},{9,... | collective-permute-start | bytes 1671176 | tf_op jit(solution)/shard_map/ppermute | solution.py:36
  15.9 5.0 %collective-permute-start.1 = (bf16[2,136,1024]{2,1,0:T(8,128)(2,1)S(1)}, bf16[2,136,1024]{2,1,0:T(8,128)(2,1)S(1)}, u32[]{:S(2)}, u32[]{:S(2)}) collective-permute-start(bf16[2,136,1024]{2,1,0:T(8,128)(2,1)S(1)} %pad_maximum_fusion.1.refs_0_), channel_id=1, source_target_pairs={{0,8},{1,9},{2,10},{3,11},{4,12},{5,13},{6,14},{7,15},{8,16},{9,17... | collective-permute-start | bytes 1671176 | tf_op jit(solution)/shard_map/ppermute | solution.py:36
  20.9 4.6 %collective-permute-start.2 = (bf16[2,136,1024]{2,1,0:T(8,128)(2,1)S(1)}, bf16[2,136,1024]{2,1,0:T(8,128)(2,1)S(1)}, u32[]{:S(2)}, u32[]{:S(2)}) collective-permute-start(bf16[2,136,1024]{2,1,0:T(8,128)(2,1)S(1)} %pad_maximum_fusion.1.refs_0_), channel_id=1, source_target_pairs={{0,56},{1,57},{2,58},{3,59},{4,60},{5,61},{6,62},{7,63},{8,0},{9,1... | collective-permute-start | bytes 1671176 | tf_op jit(solution)/shard_map/ppermute | solution.py:36
  25.5 5.3 %collective-permute-start.5 = (bf16[2,136,1024]{2,1,0:T(8,128)(2,1)S(1)}, bf16[2,136,1024]{2,1,0:T(8,128)(2,1)S(1)}, u32[]{:S(2)}, u32[]{:S(2)}) collective-permute-start(bf16[2,136,1024]{2,1,0:T(8,128)(2,1)S(1)} %collective-permute-done.3.refs_3_), channel_id=1, source_target_pairs={{0,8},{1,9},{2,10},{3,11},{4,12},{5,13},{6,14},{7,15},{8,16},{9,17... | collective-permute-start | bytes 1671176 | tf_op jit(solution)/shard_map/ppermute | solution.py:36
  30.9 4.7 %collective-permute-start.6 = (bf16[2,136,1024]{2,1,0:T(8,128)(2,1)S(1)}, bf16[2,136,1024]{2,1,0:T(8,128)(2,1)}, u32[]{:S(2)}, u32[]{:S(2)}) collective-permute-start(bf16[2,136,1024]{2,1,0:T(8,128)(2,1)S(1)} %collective-permute-done.4.refs_4_), channel_id=1, source_target_pairs={{0,56},{1,57},{2,58},{3,59},{4,60},{5,61},{6,62},{7,63},{8,0},{9,1... | collective-permute-start | bytes 1671176 | tf_op jit(solution)/shard_map/ppermute | solution.py:36
  35.6 3.5 %collective-permute-start.7 = (bf16[2,136,1024]{2,1,0:T(8,128)(2,1)S(1)}, bf16[2,136,1024]{2,1,0:T(8,128)(2,1)}, u32[]{:S(2)}, u32[]{:S(2)}) collective-permute-start(bf16[2,136,1024]{2,1,0:T(8,128)(2,1)S(1)} %collective-permute-done.3.refs_3_), channel_id=1, source_target_pairs={{0,16},{1,17},{2,18},{3,19},{4,20},{5,21},{6,22},{7,23},{8,24},{9,... | collective-permute-start | bytes 1671176 | tf_op jit(solution)/shard_map/ppermute | solution.py:36
  39.8 1.4 collective-permute-done.5.refs_5_
  41.1 2.2 collective-permute-done.6.refs_6_
  43.3 8.0 %collective-permute-done.7.refs_7_ = bf16[2,136,1024]{2,1,0:T(8,128)(2,1)} collective-permute-done((bf16[2,136,1024]{2,1,0:T(8,128)(2,1)S(1)}, bf16[2,136,1024]{2,1,0:T(8,128)(2,1)}, u32[]{:S(2)}, u32[]{:S(2)}) %collective-permute-start.7) | collective-permute-done | bytes 557088 | tf_op jit(solution)/shard_map/ppermute | solution.py:36
  52.0 5.6 %route.1 = (bf16[272,1024]{1,0:T(8,128)(2,1)}, bf16[272,1024]{1,0:T(8,128)(2,1)}, bf16[272,1024]{1,0:T(8,128)(2,1)}, bf16[272,1024]{1,0:T(8,128)(2,1)}, bf16[272...) custom-call(s32[8]{0:T(128)} %and_select_fusion.7.place_ref, ...), custom_call_target="tpu_custom_call" | custom-call | tf_op jit(solution)/shard_map/route/pallas_call | solution.py:182
  57.7 10.9 %collective-permute-start.11 = (bf16[272,1024]{1,0:T(8,128)(2,1)}, bf16[272,1024]{1,0:T(8,128)(2,1)S(1)}, u32[]{:S(2)}, u32[]{:S(2)}) collective-permute-start(bf16[272,1024]{1,0:T(8,128)(2,1)} %get-tuple-element.23), channel_id=1, source_target_pairs={{0,4},{1,5},{2,6},{3,7},{4,0},{5,1},{6,2},{7,3},{8,12},{9,13},{10,... | collective-permute-start | bytes 1671176 | tf_op jit(solution)/shard_map/ppermute | solution.py:36
  68.6 3.4 %collective-permute-start.8 = (bf16[272,1024]{1,0:T(8,128)(2,1)}, bf16[272,1024]{1,0:T(8,128)(2,1)S(1)}, u32[]{:S(2)}, u32[]{:S(2)}) collective-permute-start(bf16[272,1024]{1,0:T(8,128)(2,1)} %get-tuple-element.20), channel_id=1, source_target_pairs={{0,1},{1,2},{2,3},{3,4},{4,5},{5,6},{6,7},{7,0},{8,9},{9,10},{10,1... | collective-permute-start | bytes 1671176 | tf_op jit(solution)/shard_map/ppermute | solution.py:36
  72.0 3.7 %collective-permute-start.14 = (bf16[272,1024]{1,0:T(8,128)(2,1)}, bf16[272,1024]{1,0:T(8,128)(2,1)S(1)}, u32[]{:S(2)}, u32[]{:S(2)}) collective-permute-start(bf16[272,1024]{1,0:T(8,128)(2,1)} %get-tuple-element.26), channel_id=1, source_target_pairs={{0,7},{1,0},{2,1},{3,2},{4,3},{5,4},{6,5},{7,6},{8,15},{9,8},{10,9... | collective-permute-start | bytes 1671176 | tf_op jit(solution)/shard_map/ppermute | solution.py:36
  75.7 1.7 bitcast_dynamic-update-slice_fusion
  77.4 4.0 %collective-permute-start.10 = (bf16[272,1024]{1,0:T(8,128)(2,1)}, bf16[272,1024]{1,0:T(8,128)(2,1)S(1)}, u32[]{:S(2)}, u32[]{:S(2)}) collective-permute-start(bf16[272,1024]{1,0:T(8,128)(2,1)} %get-tuple-element.22), channel_id=1, source_target_pairs={{0,3},{1,4},{2,5},{3,6},{4,7},{5,0},{6,1},{7,2},{8,11},{9,12},{10,... | collective-permute-start | bytes 1671176 | tf_op jit(solution)/shard_map/ppermute | solution.py:36
  81.4 1.9 collective-permute-start.9
  83.4 6.6 %collective-permute-start.12 = (bf16[272,1024]{1,0:T(8,128)(2,1)}, bf16[272,1024]{1,0:T(8,128)(2,1)S(1)}, u32[]{:S(2)}, u32[]{:S(2)}) collective-permute-start(bf16[272,1024]{1,0:T(8,128)(2,1)} %get-tuple-element.24), channel_id=1, source_target_pairs={{0,5},{1,6},{2,7},{3,0},{4,1},{5,2},{6,3},{7,4},{8,13},{9,14},{10,... | collective-permute-start | bytes 1671176 | tf_op jit(solution)/shard_map/ppermute | solution.py:36
  90.7 2.8 %collective-permute-done.8.refs_1_ = bf16[272,1024]{1,0:T(8,128)(2,1)S(1)} collective-permute-done((bf16[272,1024]{1,0:T(8,128)(2,1)}, bf16[272,1024]{1,0:T(8,128)(2,1)S(1)}, u32[]{:S(2)}, u32[]{:S(2)}) %collective-permute-start.8) | collective-permute-done | bytes 557088 | tf_op jit(solution)/shard_map/ppermute | solution.py:36
  95.1 16.6 %collective-permute-done.10.refs_3_ = bf16[272,1024]{1,0:T(8,128)(2,1)S(1)} collective-permute-done((bf16[272,1024]{1,0:T(8,128)(2,1)}, bf16[272,1024]{1,0:T(8,128)(2,1)S(1)}, u32[]{:S(2)}, u32[]{:S(2)}) %collective-permute-start.10) | collective-permute-done | bytes 557088 | tf_op jit(solution)/shard_map/ppermute | solution.py:36
  112.4 5.5 %collective-permute-done.9.refs_2_ = bf16[272,1024]{1,0:T(8,128)(2,1)S(1)} collective-permute-done((bf16[272,1024]{1,0:T(8,128)(2,1)}, bf16[272,1024]{1,0:T(8,128)(2,1)S(1)}, u32[]{:S(2)}, u32[]{:S(2)}) %collective-permute-start.9) | collective-permute-done | bytes 557088 | tf_op jit(solution)/shard_map/ppermute | solution.py:36
  118.7 3.6 %collective-permute-start.15 = (bf16[6,128,1024]{2,1,0:T(8,128)(2,1)}, bf16[6,128,1024]{2,1,0:T(8,128)(2,1)}, u32[]{:S(2)}, u32[]{:S(2)}) collective-permute-start(bf16[6,128,1024]{2,1,0:T(8,128)(2,1)} %fusion.17), channel_id=1, source_target_pairs={{0,64},{64,0},{128,192},{192,128},{256,320},{320,256},{384,448},{4... | collective-permute-start | bytes 4718600 | tf_op jit(solution)/shard_map/ppermute | solution.py:26
  122.3 3.7 %collective-permute-start.13 = (bf16[272,1024]{1,0:T(8,128)(2,1)S(1)}, bf16[272,1024]{1,0:T(8,128)(2,1)S(1)}, u32[]{:S(2)}, u32[]{:S(2)}) collective-permute-start(bf16[272,1024]{1,0:T(8,128)(2,1)S(1)} %copy-done.24), channel_id=1, source_target_pairs={{0,6},{1,7},{2,0},{3,1},{4,2},{5,3},{6,4},{7,5},{8,14},{9,15},{10,... | collective-permute-start | bytes 1671176 | tf_op jit(solution)/shard_map/ppermute | solution.py:36
  126.0 4.7 %collective-permute-start.17 = (bf16[256,704]{0,1:T(8,128)(2,1)S(1)}, bf16[256,704]{0,1:T(8,128)(2,1)S(1)}, u32[]{:S(2)}, u32[]{:S(2)}) collective-permute-start(bf16[256,704]{0,1:T(8,128)(2,1)S(1)} %bitcast.78), channel_id=1, source_target_pairs={{0,384},{64,448},{128,0},{192,64},{256,128},{320,192},{384,256},{4... | collective-permute-start | bytes 1081352 | tf_op jit(solution)/shard_map/ppermute | solution.py:22
  130.6 2.7 %collective-permute-start.18 = (bf16[256,704]{0,1:T(8,128)(2,1)S(1)}, bf16[256,704]{0,1:T(8,128)(2,1)S(1)}, u32[]{:S(2)}, u32[]{:S(2)}) collective-permute-start(bf16[256,704]{0,1:T(8,128)(2,1)S(1)} %bitcast.79), channel_id=1, source_target_pairs={{0,256},{64,320},{128,384},{192,448},{256,0},{320,64},{384,128},{4... | collective-permute-start | bytes 1081352 | tf_op jit(solution)/shard_map/ppermute | solution.py:22
  133.4 2.8 %collective-permute-start.19 = (bf16[256,704]{0,1:T(8,128)(2,1)S(1)}, bf16[256,704]{0,1:T(8,128)(2,1)S(1)}, u32[]{:S(2)}, u32[]{:S(2)}) collective-permute-start(bf16[256,704]{0,1:T(8,128)(2,1)S(1)} %bitcast.80), channel_id=1, source_target_pairs={{0,128},{64,192},{128,256},{192,320},{256,384},{320,448},{384,0},{... | collective-permute-start | bytes 1081352 | tf_op jit(solution)/shard_map/ppermute | solution.py:22
  136.2 3.8 %collective-permute-done.13.refs_6_ = bf16[272,1024]{1,0:T(8,128)(2,1)S(1)} collective-permute-done((bf16[272,1024]{1,0:T(8,128)(2,1)S(1)}, bf16[272,1024]{1,0:T(8,128)(2,1)S(1)}, u32[]{:S(2)}, u32[]{:S(2)}) %collective-permute-start.13) | collective-permute-done | bytes 557088 | tf_op jit(solution)/shard_map/ppermute | solution.py:36
  141.0 1.9 collective-permute-start.16
  142.9 1.6 collective-permute-done.17
  145.4 4.8 %collective-permute-done.19 = bf16[256,704]{0,1:T(8,128)(2,1)S(1)} collective-permute-done((bf16[256,704]{0,1:T(8,128)(2,1)S(1)}, bf16[256,704]{0,1:T(8,128)(2,1)S(1)}, u32[]{:S(2)}, u32[]{:S(2)}) %collective-permute-start.19) | collective-permute-done | bytes 360480 | tf_op jit(solution)/shard_map/ppermute | solution.py:22
  150.2 1.3 pad_maximum_fusion
  151.4 1.9 collective-permute-start.20
  154.3 6.8 %join.1 = (bf16[1024,2048]{1,0:T(8,128)(2,1)}, bf16[1024,2048]{1,0:T(8,128)(2,1)}, bf16[1024,128]{1,0:T(8,128)(2,1)}) custom-call(s32[2,64]{1,0:T(2,128)} %pad_add_fusion.slots_ref, bf16[272,1024]{1,0:T(8,128)(2,1)} %get-tuple-element.19.refs_0_, bf16[272,1024]{1,0:T(8,128)(2,1)} %copy-done.9, bf16[272,1024]{1,0:T(8,128)(2,1)} %copy-done.12, ...), custom_call_target="tpu_custom_call" | custom-call | tf_op jit(solution)/shard_map/join/pallas_call | solution.py:198
  161.1 3.7 %fusion.10 = bf16[1024,704]{0,1:T(8,128)(2,1)S(1)} fusion(bf16[1024,704]{0,1:T(8,128)(2,1)} %param.9, bf16[1024,2048]{1,0:T(8,128)(2,1)} %get-tuple-element.29), kind=kOutput, calls=%fused_computation.9 | convolution fusion | flops 1477115904 | bytes 4980736 | tf_op jit(solution)/shard_map/dot_general | solution.py:214
  164.9 2.5 %collective-permute-start.21 = (bf16[4,256,704]{1,2,0:T(8,128)(2,1)S(1)}, bf16[4,256,704]{1,2,0:T(8,128)(2,1)S(1)}, u32[]{:S(2)}, u32[]{:S(2)}) collective-permute-start(bf16[4,256,704]{1,2,0:T(8,128)(2,1)S(1)} %bitcast.76), channel_id=1, source_target_pairs={{0,64},{64,0},{128,192},{192,128},{256,320},{320,256},{384,448},{4... | collective-permute-start | bytes 4325384 | tf_op jit(solution)/shard_map/ppermute | solution.py:26
  167.6 1.5 constant_dynamic-update-slice_fusion
  171.8 1.7 fusion.7
  175.0 2.8 %collective-permute-start.22 = (bf16[256,704]{0,1:T(8,128)(2,1)}, bf16[256,704]{0,1:T(8,128)(2,1)S(1)}, u32[]{:S(2)}, u32[]{:S(2)}) collective-permute-start(bf16[256,704]{0,1:T(8,128)(2,1)} %get-tuple-element.35), channel_id=1, source_target_pairs={{0,256},{64,320},{128,384},{192,448},{256,0},{320,64},{384,128},{4... | collective-permute-start | bytes 1081352 | tf_op jit(solution)/shard_map/ppermute | solution.py:22
  177.8 2.6 %collective-permute-start.23 = (bf16[256,704]{0,1:T(8,128)(2,1)}, bf16[256,704]{0,1:T(8,128)(2,1)}, u32[]{:S(2)}, u32[]{:S(2)}) collective-permute-start(bf16[256,704]{0,1:T(8,128)(2,1)} %get-tuple-element.37), channel_id=1, source_target_pairs={{0,128},{64,192},{128,256},{192,320},{256,384},{320,448},{384,0},{... | collective-permute-start | bytes 1081352 | tf_op jit(solution)/shard_map/ppermute | solution.py:22
  180.4 4.5 %collective-permute-start.24 = (bf16[256,704]{0,1:T(8,128)(2,1)}, bf16[256,704]{0,1:T(8,128)(2,1)}, u32[]{:S(2)}, u32[]{:S(2)}) collective-permute-start(bf16[256,704]{0,1:T(8,128)(2,1)} %get-tuple-element.36), channel_id=1, source_target_pairs={{0,384},{64,448},{128,0},{192,64},{256,128},{320,192},{384,256},{4... | collective-permute-start | bytes 1081352 | tf_op jit(solution)/shard_map/ppermute | solution.py:22
  184.9 4.4 %multiply_reduce_fusion = (f32[1024]{0:T(1024)S(1)}, bf16[1024,704]{0,1:T(8,128)(2,1)}) fusion(bf16[1024,704]{0,1:T(8,128)(2,1)S(1)} %copy-done.23, f32[1024]{0:T(1024)S(1)} %convert_reduce_fusion, bf16[1024,2048]{1,0:T(8,128)(2,1)S(1)} %copy-done.21, bf16[2048,704]{0,1:T(8,128)(2,1)S(1)} %bitcast.74), kind=kOutput, calls=%fused_computation.1 | convolution fusion | flops 2956393472 | bytes 9969664 | tf_op jit(solution)/shard_map/dot_general | solution.py:225
  189.4 26.1 %all_to_all.11 = f32[64,1,16]{2,1,0:T(1,128)} all-to-all(f32[64,1,16]{2,1,0:T(1,128)S(1)} %bitcast.87), channel_id=1, replica_groups=mesh['dp'=8,'expert'=64] {'expert'}, dimensions={0} | all-to-all | bytes 8192 | tf_op jit(solution)/shard_map/all_to_all | solution.py:40
  215.5 1.6 pick.1
  217.2 1.3 slice_bitcast_fusion.11
  218.4 2.1 fusion.16
  (96 shorter events, 13.9 us)
Async XLA Ops:
  0.6 38.5 %copy-start.25 = (s32[8]{0:T(128)S(1)}, s32[8]{0:T(128)}, u32[]{:S(2)}) copy-start(s32[8]{0:T(128)} %constant.148.clone) | copy-start | bytes 100
  3.2 3.7 %collective-permute-start = (bf16[136,1024]{1,0:T(8,128)(2,1)}, bf16[136,1024]{1,0:T(8,128)(2,1)S(1)}, u32[]{:S(2)}, u32[]{:S(2)}) collective-permute-start(bf16[136,1024]{1,0:T(8,128)(2,1)} %get-tuple-element.18), channel_id=1, source_target_pairs={{0,64},{64,0},{128,192},{192,128},{256,320},{320,256},{384,448},{4... | collective-permute-start | bytes 835592 | tf_op jit(solution)/shard_map/ppermute | solution.py:26
  7.9 44.1 %copy-start = (bf16[2,136,1024]{2,1,0:T(8,128)(2,1)}, bf16[2,136,1024]{2,1,0:T(8,128)(2,1)S(1)}, u32[]{:S(2)}) copy-start(bf16[2,136,1024]{2,1,0:T(8,128)(2,1)S(1)} %pad_maximum_fusion.1.refs_0_) | copy-start | bytes 1671172
  7.9 17.6 %collective-permute-start.3 = (bf16[2,136,1024]{2,1,0:T(8,128)(2,1)S(1)}, bf16[2,136,1024]{2,1,0:T(8,128)(2,1)S(1)}, u32[]{:S(2)}, u32[]{:S(2)}) collective-permute-start(bf16[2,136,1024]{2,1,0:T(8,128)(2,1)S(1)} %pad_maximum_fusion.1.refs_0_), channel_id=1, source_target_pairs={{0,16},{1,17},{2,18},{3,19},{4,20},{5,21},{6,22},{7,23},{8,24},{9,... | collective-permute-start | bytes 1671176 | tf_op jit(solution)/shard_map/ppermute | solution.py:36
  12.4 18.5 %collective-permute-start.4 = (bf16[2,136,1024]{2,1,0:T(8,128)(2,1)S(1)}, bf16[2,136,1024]{2,1,0:T(8,128)(2,1)S(1)}, u32[]{:S(2)}, u32[]{:S(2)}) collective-permute-start(bf16[2,136,1024]{2,1,0:T(8,128)(2,1)S(1)} %pad_maximum_fusion.1.refs_0_), channel_id=1, source_target_pairs={{0,48},{1,49},{2,50},{3,51},{4,52},{5,53},{6,54},{7,55},{8,56},{9,... | collective-permute-start | bytes 1671176 | tf_op jit(solution)/shard_map/ppermute | solution.py:36
  15.9 23.9 %collective-permute-start.1 = (bf16[2,136,1024]{2,1,0:T(8,128)(2,1)S(1)}, bf16[2,136,1024]{2,1,0:T(8,128)(2,1)S(1)}, u32[]{:S(2)}, u32[]{:S(2)}) collective-permute-start(bf16[2,136,1024]{2,1,0:T(8,128)(2,1)S(1)} %pad_maximum_fusion.1.refs_0_), channel_id=1, source_target_pairs={{0,8},{1,9},{2,10},{3,11},{4,12},{5,13},{6,14},{7,15},{8,16},{9,17... | collective-permute-start | bytes 1671176 | tf_op jit(solution)/shard_map/ppermute | solution.py:36
  20.9 18.8 %collective-permute-start.2 = (bf16[2,136,1024]{2,1,0:T(8,128)(2,1)S(1)}, bf16[2,136,1024]{2,1,0:T(8,128)(2,1)S(1)}, u32[]{:S(2)}, u32[]{:S(2)}) collective-permute-start(bf16[2,136,1024]{2,1,0:T(8,128)(2,1)S(1)} %pad_maximum_fusion.1.refs_0_), channel_id=1, source_target_pairs={{0,56},{1,57},{2,58},{3,59},{4,60},{5,61},{6,62},{7,63},{8,0},{9,1... | collective-permute-start | bytes 1671176 | tf_op jit(solution)/shard_map/ppermute | solution.py:36
  25.5 26.5 %copy-start.15 = (bf16[2,136,1024]{2,1,0:T(8,128)(2,1)}, bf16[2,136,1024]{2,1,0:T(8,128)(2,1)S(1)}, u32[]{:S(2)}) copy-start(bf16[2,136,1024]{2,1,0:T(8,128)(2,1)S(1)} %collective-permute-done.3.refs_3_) | copy-start | bytes 1671172
  25.5 15.6 %collective-permute-start.5 = (bf16[2,136,1024]{2,1,0:T(8,128)(2,1)S(1)}, bf16[2,136,1024]{2,1,0:T(8,128)(2,1)S(1)}, u32[]{:S(2)}, u32[]{:S(2)}) collective-permute-start(bf16[2,136,1024]{2,1,0:T(8,128)(2,1)S(1)} %collective-permute-done.3.refs_3_), channel_id=1, source_target_pairs={{0,8},{1,9},{2,10},{3,11},{4,12},{5,13},{6,14},{7,15},{8,16},{9,17... | collective-permute-start | bytes 1671176 | tf_op jit(solution)/shard_map/ppermute | solution.py:36
  30.9 21.1 %copy-start.16 = (bf16[2,136,1024]{2,1,0:T(8,128)(2,1)}, bf16[2,136,1024]{2,1,0:T(8,128)(2,1)S(1)}, u32[]{:S(2)}) copy-start(bf16[2,136,1024]{2,1,0:T(8,128)(2,1)S(1)} %collective-permute-done.4.refs_4_) | copy-start | bytes 1671172
  30.9 12.4 %collective-permute-start.6 = (bf16[2,136,1024]{2,1,0:T(8,128)(2,1)S(1)}, bf16[2,136,1024]{2,1,0:T(8,128)(2,1)}, u32[]{:S(2)}, u32[]{:S(2)}) collective-permute-start(bf16[2,136,1024]{2,1,0:T(8,128)(2,1)S(1)} %collective-permute-done.4.refs_4_), channel_id=1, source_target_pairs={{0,56},{1,57},{2,58},{3,59},{4,60},{5,61},{6,62},{7,63},{8,0},{9,1... | collective-permute-start | bytes 1671176 | tf_op jit(solution)/shard_map/ppermute | solution.py:36
  35.6 15.7 %collective-permute-start.7 = (bf16[2,136,1024]{2,1,0:T(8,128)(2,1)S(1)}, bf16[2,136,1024]{2,1,0:T(8,128)(2,1)}, u32[]{:S(2)}, u32[]{:S(2)}) collective-permute-start(bf16[2,136,1024]{2,1,0:T(8,128)(2,1)S(1)} %collective-permute-done.3.refs_3_), channel_id=1, source_target_pairs={{0,16},{1,17},{2,18},{3,19},{4,20},{5,21},{6,22},{7,23},{8,24},{9,... | collective-permute-start | bytes 1671176 | tf_op jit(solution)/shard_map/ppermute | solution.py:36
  39.7 12.3 %copy-start.17 = (bf16[2,136,1024]{2,1,0:T(8,128)(2,1)}, bf16[2,136,1024]{2,1,0:T(8,128)(2,1)S(1)}, u32[]{:S(2)}) copy-start(bf16[2,136,1024]{2,1,0:T(8,128)(2,1)S(1)} %collective-permute-done.1.refs_1_) | copy-start | bytes 1671172
  39.7 12.3 %copy-start.18 = (bf16[2,136,1024]{2,1,0:T(8,128)(2,1)}, bf16[2,136,1024]{2,1,0:T(8,128)(2,1)S(1)}, u32[]{:S(2)}) copy-start(bf16[2,136,1024]{2,1,0:T(8,128)(2,1)S(1)} %collective-permute-done.2.refs_2_) | copy-start | bytes 1671172
  41.1 10.9 %copy-start.19 = (bf16[2,136,1024]{2,1,0:T(8,128)(2,1)}, bf16[2,136,1024]{2,1,0:T(8,128)(2,1)S(1)}, u32[]{:S(2)}) copy-start(bf16[2,136,1024]{2,1,0:T(8,128)(2,1)S(1)} %collective-permute-done.5.refs_5_) | copy-start | bytes 1671172
  57.7 25.7 %collective-permute-start.11 = (bf16[272,1024]{1,0:T(8,128)(2,1)}, bf16[272,1024]{1,0:T(8,128)(2,1)S(1)}, u32[]{:S(2)}, u32[]{:S(2)}) collective-permute-start(bf16[272,1024]{1,0:T(8,128)(2,1)} %get-tuple-element.23), channel_id=1, source_target_pairs={{0,4},{1,5},{2,6},{3,7},{4,0},{5,1},{6,2},{7,3},{8,12},{9,13},{10,... | collective-permute-start | bytes 1671176 | tf_op jit(solution)/shard_map/ppermute | solution.py:36
  68.6 24.9 %collective-permute-start.8 = (bf16[272,1024]{1,0:T(8,128)(2,1)}, bf16[272,1024]{1,0:T(8,128)(2,1)S(1)}, u32[]{:S(2)}, u32[]{:S(2)}) collective-permute-start(bf16[272,1024]{1,0:T(8,128)(2,1)} %get-tuple-element.20), channel_id=1, source_target_pairs={{0,1},{1,2},{2,3},{3,4},{4,5},{5,6},{6,7},{7,0},{8,9},{9,10},{10,1... | collective-permute-start | bytes 1671176 | tf_op jit(solution)/shard_map/ppermute | solution.py:36
  72.0 22.3 %collective-permute-start.14 = (bf16[272,1024]{1,0:T(8,128)(2,1)}, bf16[272,1024]{1,0:T(8,128)(2,1)S(1)}, u32[]{:S(2)}, u32[]{:S(2)}) collective-permute-start(bf16[272,1024]{1,0:T(8,128)(2,1)} %get-tuple-element.26), channel_id=1, source_target_pairs={{0,7},{1,0},{2,1},{3,2},{4,3},{5,4},{6,5},{7,6},{8,15},{9,8},{10,9... | collective-permute-start | bytes 1671176 | tf_op jit(solution)/shard_map/ppermute | solution.py:36
  75.7 46.6 %copy-start.24 = (bf16[272,1024]{1,0:T(8,128)(2,1)S(1)}, bf16[272,1024]{1,0:T(8,128)(2,1)}, u32[]{:S(2)}) copy-start(bf16[272,1024]{1,0:T(8,128)(2,1)} %get-tuple-element.25) | copy-start | bytes 1671172
  75.7 50.3 %copy-start.1 = (bf16[1,256,704]{1,2,0:T(8,128)(2,1)S(1)}, bf16[1,256,704]{1,2,0:T(8,128)(2,1)}, u32[]{:S(2)}) copy-start(bf16[1,256,704]{1,2,0:T(8,128)(2,1)} %param.10) | copy-start | bytes 1081348
  77.4 34.2 %collective-permute-start.10 = (bf16[272,1024]{1,0:T(8,128)(2,1)}, bf16[272,1024]{1,0:T(8,128)(2,1)S(1)}, u32[]{:S(2)}, u32[]{:S(2)}) collective-permute-start(bf16[272,1024]{1,0:T(8,128)(2,1)} %get-tuple-element.22), channel_id=1, source_target_pairs={{0,3},{1,4},{2,5},{3,6},{4,7},{5,0},{6,1},{7,2},{8,11},{9,12},{10,... | collective-permute-start | bytes 1671176 | tf_op jit(solution)/shard_map/ppermute | solution.py:36
  81.4 36.5 %collective-permute-start.9 = (bf16[272,1024]{1,0:T(8,128)(2,1)}, bf16[272,1024]{1,0:T(8,128)(2,1)S(1)}, u32[]{:S(2)}, u32[]{:S(2)}) collective-permute-start(bf16[272,1024]{1,0:T(8,128)(2,1)} %get-tuple-element.21), channel_id=1, source_target_pairs={{0,2},{1,3},{2,4},{3,5},{4,6},{5,7},{6,0},{7,1},{8,10},{9,11},{10,... | collective-permute-start | bytes 1671176 | tf_op jit(solution)/shard_map/ppermute | solution.py:36
  83.4 52.9 %copy-start.8 = (bf16[272,1024]{1,0:T(8,128)(2,1)}, bf16[272,1024]{1,0:T(8,128)(2,1)S(1)}, u32[]{:S(2)}) copy-start(bf16[272,1024]{1,0:T(8,128)(2,1)S(1)} %collective-permute-done.11.refs_4_) | copy-start | bytes 1671172
  83.4 50.0 %collective-permute-start.12 = (bf16[272,1024]{1,0:T(8,128)(2,1)}, bf16[272,1024]{1,0:T(8,128)(2,1)S(1)}, u32[]{:S(2)}, u32[]{:S(2)}) collective-permute-start(bf16[272,1024]{1,0:T(8,128)(2,1)} %get-tuple-element.24), channel_id=1, source_target_pairs={{0,5},{1,6},{2,7},{3,0},{4,1},{5,2},{6,3},{7,4},{8,13},{9,14},{10,... | collective-permute-start | bytes 1671176 | tf_op jit(solution)/shard_map/ppermute | solution.py:36
  93.5 46.6 %copy-start.9 = (bf16[272,1024]{1,0:T(8,128)(2,1)}, bf16[272,1024]{1,0:T(8,128)(2,1)S(1)}, u32[]{:S(2)}) copy-start(bf16[272,1024]{1,0:T(8,128)(2,1)S(1)} %collective-permute-done.8.refs_1_) | copy-start | bytes 1671172
  94.3 45.8 %copy-start.10 = (bf16[272,1024]{1,0:T(8,128)(2,1)}, bf16[272,1024]{1,0:T(8,128)(2,1)S(1)}, u32[]{:S(2)}) copy-start(bf16[272,1024]{1,0:T(8,128)(2,1)S(1)} %collective-permute-done.14.refs_7_) | copy-start | bytes 1671172
  111.7 29.4 %copy-start.11 = (bf16[272,1024]{1,0:T(8,128)(2,1)}, bf16[272,1024]{1,0:T(8,128)(2,1)S(1)}, u32[]{:S(2)}) copy-start(bf16[272,1024]{1,0:T(8,128)(2,1)S(1)} %collective-permute-done.10.refs_3_) | copy-start | bytes 1671172
  117.9 32.2 %copy-start.12 = (bf16[272,1024]{1,0:T(8,128)(2,1)}, bf16[272,1024]{1,0:T(8,128)(2,1)S(1)}, u32[]{:S(2)}) copy-start(bf16[272,1024]{1,0:T(8,128)(2,1)S(1)} %collective-permute-done.9.refs_2_) | copy-start | bytes 1671172
  118.7 35.6 %collective-permute-start.15 = (bf16[6,128,1024]{2,1,0:T(8,128)(2,1)}, bf16[6,128,1024]{2,1,0:T(8,128)(2,1)}, u32[]{:S(2)}, u32[]{:S(2)}) collective-permute-start(bf16[6,128,1024]{2,1,0:T(8,128)(2,1)} %fusion.17), channel_id=1, source_target_pairs={{0,64},{64,0},{128,192},{192,128},{256,320},{320,256},{384,448},{4... | collective-permute-start | bytes 4718600 | tf_op jit(solution)/shard_map/ppermute | solution.py:26
  122.3 17.8 %collective-permute-start.13 = (bf16[272,1024]{1,0:T(8,128)(2,1)S(1)}, bf16[272,1024]{1,0:T(8,128)(2,1)S(1)}, u32[]{:S(2)}, u32[]{:S(2)}) collective-permute-start(bf16[272,1024]{1,0:T(8,128)(2,1)S(1)} %copy-done.24), channel_id=1, source_target_pairs={{0,6},{1,7},{2,0},{3,1},{4,2},{5,3},{6,4},{7,5},{8,14},{9,15},{10,... | collective-permute-start | bytes 1671176 | tf_op jit(solution)/shard_map/ppermute | solution.py:36
  126.0 18.6 %collective-permute-start.17 = (bf16[256,704]{0,1:T(8,128)(2,1)S(1)}, bf16[256,704]{0,1:T(8,128)(2,1)S(1)}, u32[]{:S(2)}, u32[]{:S(2)}) collective-permute-start(bf16[256,704]{0,1:T(8,128)(2,1)S(1)} %bitcast.78), channel_id=1, source_target_pairs={{0,384},{64,448},{128,0},{192,64},{256,128},{320,192},{384,256},{4... | collective-permute-start | bytes 1081352 | tf_op jit(solution)/shard_map/ppermute | solution.py:22
  130.6 14.7 %collective-permute-start.18 = (bf16[256,704]{0,1:T(8,128)(2,1)S(1)}, bf16[256,704]{0,1:T(8,128)(2,1)S(1)}, u32[]{:S(2)}, u32[]{:S(2)}) collective-permute-start(bf16[256,704]{0,1:T(8,128)(2,1)S(1)} %bitcast.79), channel_id=1, source_target_pairs={{0,256},{64,320},{128,384},{192,448},{256,0},{320,64},{384,128},{4... | collective-permute-start | bytes 1081352 | tf_op jit(solution)/shard_map/ppermute | solution.py:22
  133.4 16.8 %copy-start.13 = (bf16[272,1024]{1,0:T(8,128)(2,1)}, bf16[272,1024]{1,0:T(8,128)(2,1)S(1)}, u32[]{:S(2)}) copy-start(bf16[272,1024]{1,0:T(8,128)(2,1)S(1)} %collective-permute-done.12.refs_5_) | copy-start | bytes 1671172
  133.4 16.7 %collective-permute-start.19 = (bf16[256,704]{0,1:T(8,128)(2,1)S(1)}, bf16[256,704]{0,1:T(8,128)(2,1)S(1)}, u32[]{:S(2)}, u32[]{:S(2)}) collective-permute-start(bf16[256,704]{0,1:T(8,128)(2,1)S(1)} %bitcast.80), channel_id=1, source_target_pairs={{0,128},{64,192},{128,256},{192,320},{256,384},{320,448},{384,0},{... | collective-permute-start | bytes 1081352 | tf_op jit(solution)/shard_map/ppermute | solution.py:22
  140.1 10.1 %copy-start.14 = (bf16[272,1024]{1,0:T(8,128)(2,1)}, bf16[272,1024]{1,0:T(8,128)(2,1)S(1)}, u32[]{:S(2)}) copy-start(bf16[272,1024]{1,0:T(8,128)(2,1)S(1)} %collective-permute-done.13.refs_6_) | copy-start | bytes 1671172
  141.0 13.2 %collective-permute-start.16 = (bf16[2,128,1024]{2,1,0:T(8,128)(2,1)}, bf16[2,128,1024]{2,1,0:T(8,128)(2,1)}, u32[]{:S(2)}, u32[]{:S(2)}) collective-permute-start(bf16[2,128,1024]{2,1,0:T(8,128)(2,1)} %pad_maximum_fusion.2), channel_id=1, source_target_pairs={{0,64},{64,0},{128,192},{192,128},{256,320},{320,256},{384,448},{4... | collective-permute-start | bytes 1572872 | tf_op jit(solution)/shard_map/ppermute | solution.py:26
  144.5 5.6 %copy-start.2 = (bf16[256,704]{0,1:T(8,128)(2,1)}, bf16[256,704]{0,1:T(8,128)(2,1)S(1)}, u32[]{:S(2)}) copy-start(bf16[256,704]{0,1:T(8,128)(2,1)S(1)} %collective-permute-done.17) | copy-start | bytes 1081348
  145.3 6.1 %copy-start.4 = (bf16[256,704]{0,1:T(8,128)(2,1)}, bf16[256,704]{0,1:T(8,128)(2,1)S(1)}, u32[]{:S(2)}) copy-start(bf16[256,704]{0,1:T(8,128)(2,1)S(1)} %collective-permute-done.18) | copy-start | bytes 1081348
  150.1 3.2 %copy-start.6 = (bf16[256,704]{0,1:T(8,128)(2,1)}, bf16[256,704]{0,1:T(8,128)(2,1)S(1)}, u32[]{:S(2)}) copy-start(bf16[256,704]{0,1:T(8,128)(2,1)S(1)} %collective-permute-done.19) | copy-start | bytes 1081348
  151.4 16.1 %collective-permute-start.20 = (bf16[4,256,704]{1,2,0:T(8,128)(2,1)}, bf16[4,256,704]{1,2,0:T(8,128)(2,1)}, u32[]{:S(2)}, u32[]{:S(2)}) collective-permute-start(bf16[4,256,704]{1,2,0:T(8,128)(2,1)} %pad_maximum_fusion), channel_id=1, source_target_pairs={{0,64},{64,0},{128,192},{192,128},{256,320},{320,256},{384,448},{4... | collective-permute-start | bytes 4325384 | tf_op jit(solution)/shard_map/ppermute | solution.py:26
  164.8 2.7 %copy-start.5 = (bf16[256,704]{0,1:T(8,128)(2,1)S(1)}, bf16[256,704]{0,1:T(8,128)(2,1)}, u32[]{:S(2)}) copy-start(bf16[256,704]{0,1:T(8,128)(2,1)} %copy-done.4) | copy-start | bytes 1081348
  164.8 2.7 %copy-start.7 = (bf16[256,704]{0,1:T(8,128)(2,1)S(1)}, bf16[256,704]{0,1:T(8,128)(2,1)}, u32[]{:S(2)}) copy-start(bf16[256,704]{0,1:T(8,128)(2,1)} %copy-done.6) | copy-start | bytes 1081348
  164.9 8.6 %collective-permute-start.21 = (bf16[4,256,704]{1,2,0:T(8,128)(2,1)S(1)}, bf16[4,256,704]{1,2,0:T(8,128)(2,1)S(1)}, u32[]{:S(2)}, u32[]{:S(2)}) collective-permute-start(bf16[4,256,704]{1,2,0:T(8,128)(2,1)S(1)} %bitcast.76), channel_id=1, source_target_pairs={{0,64},{64,0},{128,192},{192,128},{256,320},{320,256},{384,448},{4... | collective-permute-start | bytes 4325384 | tf_op jit(solution)/shard_map/ppermute | solution.py:26
  169.1 2.7 %copy-start.23 = (bf16[1024,704]{0,1:T(8,128)(2,1)S(1)}, bf16[1024,704]{0,1:T(8,128)(2,1)}, u32[]{:S(2)}) copy-start(bf16[1024,704]{0,1:T(8,128)(2,1)} %param.9) | copy-start | bytes 4325380
  173.5 11.4 %copy-start.21 = (bf16[1024,2048]{1,0:T(8,128)(2,1)S(1)}, bf16[1024,2048]{1,0:T(8,128)(2,1)}, u32[]{:S(2)}) copy-start(bf16[1024,2048]{1,0:T(8,128)(2,1)} %get-tuple-element.28) | copy-start | bytes 12582916
  175.0 43.4 %collective-permute-start.22 = (bf16[256,704]{0,1:T(8,128)(2,1)}, bf16[256,704]{0,1:T(8,128)(2,1)S(1)}, u32[]{:S(2)}, u32[]{:S(2)}) collective-permute-start(bf16[256,704]{0,1:T(8,128)(2,1)} %get-tuple-element.35), channel_id=1, source_target_pairs={{0,256},{64,320},{128,384},{192,448},{256,0},{320,64},{384,128},{4... | collective-permute-start | bytes 1081352 | tf_op jit(solution)/shard_map/ppermute | solution.py:22
  177.8 40.6 %collective-permute-start.23 = (bf16[256,704]{0,1:T(8,128)(2,1)}, bf16[256,704]{0,1:T(8,128)(2,1)}, u32[]{:S(2)}, u32[]{:S(2)}) collective-permute-start(bf16[256,704]{0,1:T(8,128)(2,1)} %get-tuple-element.37), channel_id=1, source_target_pairs={{0,128},{64,192},{128,256},{192,320},{256,384},{320,448},{384,0},{... | collective-permute-start | bytes 1081352 | tf_op jit(solution)/shard_map/ppermute | solution.py:22
  180.4 38.0 %collective-permute-start.24 = (bf16[256,704]{0,1:T(8,128)(2,1)}, bf16[256,704]{0,1:T(8,128)(2,1)}, u32[]{:S(2)}, u32[]{:S(2)}) collective-permute-start(bf16[256,704]{0,1:T(8,128)(2,1)} %get-tuple-element.36), channel_id=1, source_target_pairs={{0,384},{64,448},{128,0},{192,64},{256,128},{320,192},{384,256},{4... | collective-permute-start | bytes 1081352 | tf_op jit(solution)/shard_map/ppermute | solution.py:22
  (3 other events, 5.9 us)

commit v2 on v1

--- a/solution.py
+++ b/solution.py
@@ -13,7 +13,7 @@
 LANES = 128
 TOP = 6
 OFFSETS = [0, -1, 1, -2, 2, -3, 3, -4]
-EARLY, LATE = [0, 4, 1, 7, 3, 2], [6, 5]
+EARLY, LATE = [0, 4, 1, 7, 3, 5], [6, 2]
 VMEM = pl.BlockSpec(memory_space=pltpu.VMEM)
 SMEM = pl.BlockSpec(memory_space=pltpu.SMEM)
 
@@ -40,7 +40,7 @@
     return lax.all_to_all(a, "expert", split_axis=0, concat_axis=0, tiled=True)
 
 
-def head_kernel(place_ref, ids_ref, gates_ref, tokens_ref, own_ref, other_ref, target_ref):
+def head_kernel(ids_ref, gates_ref, tokens_ref, pair_ref, other_ref, target_ref):
     tokens, share = tokens_ref.shape[0], tokens_ref.shape[1] // (2 * CHIPS)
     experts = SIDE * SIDE
     row = lax.broadcasted_iota(jnp.int32, (tokens, tokens), 0)
@@ -53,10 +53,12 @@
     ids = jnp.concatenate([ids_ref[...].astype(jnp.float32), blank - 1.0], axis=0)
     ranks = jnp.concatenate(ranks + [blank], axis=0)
     gates = jnp.concatenate([gates_ref[...].astype(jnp.float32), blank], axis=0)
-    target_ref[...] = (ids * CAP + ranks).astype(jnp.int32)
-    for half, out_ref in enumerate((own_ref, other_ref)):
+    target_ref[...] = (ids * CAP + ranks)[0:TOP].astype(jnp.int32)
+    dp = lax.axis_index("dp")
+    for half, out_ref in enumerate((pair_ref.at[0], other_ref)):
         for b in range(CHIPS):
-            start = pl.multiple_of(place_ref[half * CHIPS + b] * share, share)
+            place = lax.rem(dp // 2 + b, CHIPS) * 2 + lax.rem(dp + half, 2)
+            start = pl.multiple_of(place * share, share)
             out_ref[0:tokens, b * share : (b + 1) * share] = tokens_ref[:, pl.ds(start, share)]
         for n, part in enumerate((ids, ranks, gates)):
             out_ref[tokens : tokens + 8, n * tokens : (n + 1) * tokens] = part.astype(jnp.bfloat16)
@@ -65,9 +67,11 @@
         )
 
 
-def route_kernel(place_ref, want_ref, *refs):
+def route_kernel(place_ref, *refs):
     blocks, outs = refs[:SIDE], refs[SIDE:]
-    want = want_ref[...]
+    line = lax.broadcasted_iota(jnp.int32, (LINE, LINE), 0)
+    step = (place_ref[SIDE] + line // CAP) % SIDE
+    want = ((step * place_ref[SIDE + 1] + place_ref[SIDE + 2]) * CAP + line % CAP).astype(jnp.float32)
     ones = jnp.ones((LINE, LANES), jnp.bfloat16)
     for d in range(SIDE):
         place = place_ref[d]
@@ -153,41 +157,45 @@
     slot_rows, units = hidden.shape
     half = width // 2
     me, dp = lax.axis_index("expert"), lax.axis_index("dp")
-    my_y, my_z, my_x, my_c = me // SIDE, me % SIDE, dp // 2, dp % 2
+    my_y, my_z, my_c = me // SIDE, me % SIDE, dp % 2
     along = jnp.where(my_c == 0, my_y, my_z)
     across = jnp.where(my_c == 0, my_z, my_y)
 
-    b = jnp.arange(2 * CHIPS, dtype=i32)
-    place = (my_x + b % CHIPS) % CHIPS * 2 + (my_c + b // CHIPS) % 2
-    block = jax.ShapeDtypeStruct((tok_rows + 8, half), bf16)
-    own, other, target = pl.pallas_call(
+    block = (tok_rows + 8, half)
+    pair, other, target = pl.pallas_call(
         head_kernel,
-        out_shape=(block, block, jax.ShapeDtypeStruct((8, tok_rows), i32)),
-        in_specs=[SMEM, VMEM, VMEM, VMEM],
+        out_shape=(
+            jax.ShapeDtypeStruct((2,) + block, bf16),
+            jax.ShapeDtypeStruct(block, bf16),
+            jax.ShapeDtypeStruct((TOP, tok_rows), i32),
+        ),
+        in_specs=[VMEM, VMEM, VMEM],
         out_specs=(VMEM,) * 3,
         name="head",
-    )(place, expert_ids.T, gates.T, grad_out)
+    )(expert_ids.T, gates.T, grad_out)
 
     lent = swap_core(other)
-    pair = jnp.stack([own, lent])
+    pair = lax.dynamic_update_slice(pair, lent[None], (1, 0, 0))
     minus_2, plus_2 = move_plane(pair, 2, 0), move_plane(pair, -2, 0)
     minus_1, plus_1 = move_plane(pair, 1, 0), move_plane(pair, -1, 0)
     minus_4 = move_plane(minus_2, 2, 0)
     minus_3, plus_3 = move_plane(minus_2, 1, 0), move_plane(plus_2, -1, 0)
     found = [pair, minus_1, plus_1, minus_2, plus_2, minus_3, plus_3, minus_4]
 
-    slot = jnp.arange(LINE, dtype=i32)
-    step, cap = (across + slot // CAP) % SIDE, slot % CAP
-    want = jnp.where(my_c == 0, my_y * SIDE + step, step * SIDE + my_z) * CAP + cap
+    stride = jnp.where(my_c == 0, 1, SIDE)
+    origin = jnp.where(my_c == 0, my_y * SIDE, my_z)
+    spots = (along + jnp.array(OFFSETS + [0] * 3, i32)) % SIDE
+    n = jnp.arange(SIDE + 3, dtype=i32)
+    spots = jnp.where(n == SIDE, across, jnp.where(n == SIDE + 1, stride, jnp.where(n == SIDE + 2, origin, spots)))
     routed = pl.pallas_call(
         route_kernel,
         out_shape=(jax.ShapeDtypeStruct((2 * LINE + CAP, half), bf16),) * SIDE,
-        in_specs=[SMEM] + [VMEM] * (SIDE + 1),
+        in_specs=[SMEM] + [VMEM] * SIDE,
         out_specs=(VMEM,) * SIDE,
         name="route",
-    )((along + jnp.array(OFFSETS, i32)) % SIDE, jnp.broadcast_to(want.astype(f32)[:, None], (LINE, tok_rows)), *found)
+    )(spots, *found)
     kept = list(routed)
-    for k in [4, 3, 5, 2, 6, 1, 7]:
+    for k in [3, 5, 4, 2, 6, 1, 7]:
         kept[k] = move_plane(routed[k], k, 1)
     early = swap_core(jnp.stack([kept[k][LINE : 2 * LINE] for k in EARLY]))
     late = swap_core(jnp.stack([kept[k][LINE : 2 * LINE] for k in LATE]))
@@ -227,7 +235,7 @@
     slot_grad = jnp.sum(hidden.astype(f32) * u_rows, axis=1)
 
     returned = exchange(slot_grad.reshape(experts, CAP))
-    grad_gates = pick(target, returned)[:TOP].T
+    grad_gates = pick(target, returned).T
     return (grad_hidden, grad_down[None], grad_gates)
 
 

time: 222 us -> 207 us (0.932)
  starting transfers between devices: 97.1 us -> 90 us
  blocking collectives: 26.1 us -> 19.3 us
    ppermute x14, starting transfers between devices: 65.2 us -> 57.2 us  [move_plane(): return lax.ppermute(a, ('dp', 'expert'), pairs)]
    all_to_all x1, blocking collectives: 26.1 us -> 19.3 us  [exchange(): return lax.all_to_all(a, 'expert', split_axis=0, concat_axis=0, tiled=True)]
    unnamed x61 -> x59, local copies, waits for them, and re-layouts: 7.14 us -> 7.93 us
  transfers between devices with their start and end apart: 25 -> 25, of which waited for: 11 -> 7; matrix products, arithmetic and copies ran while one was open for 10% -> 11% of each run, Pallas kernels for 4% -> 4%
where the time goes in v2:
time: 207 us; the launch traced here: 206 us
  starting transfers between devices  90 us (43%)
  waiting for transfers between devices  50.3 us (24%)
  blocking collectives  19.3 us (9%)
  Pallas kernels  16.2 us (8%)
  local copies, waits for them, and re-layouts  12.7 us (6%)
  matrix products  9.78 us (5%)
  other arithmetic  6.78 us (3%)
    ppermute x14, starting transfers between devices, move_plane(): return lax.ppermute(a, ('dp', 'expert'), pairs)  57.2 us
    ppermute x14, waiting for transfers between devices, move_plane(): return lax.ppermute(a, ('dp', 'expert'), pairs)  40 us
    ppermute x6, starting transfers between devices, move_x(): lax.ppermute(a, 'dp', [(x * 2 + c, (x + k) % CHIPS * 2 + c) for x in rang...  20.3 us
    all_to_all x1, blocking collectives, exchange(): return lax.all_to_all(a, 'expert', split_axis=0, concat_axis=0, tiled=True)  19.3 us
    ppermute x5, starting transfers between devices, swap_core(): lax.ppermute(a, 'dp', [(x * 2 + c, x * 2 + 1 - c) for x in range(CHIPS) f...  12.5 us
    ppermute x6, waiting for transfers between devices, move_x(): lax.ppermute(a, 'dp', [(x * 2 + c, (x + k) % CHIPS * 2 + c) for x in rang...  8.55 us
    unnamed x59, local copies, waits for them, and re-layouts  7.93 us
    pallas_call x1, Pallas kernels, shards(): pl.pallas_call(join_kernel, out_shape=(full, full, jax.ShapeDtypeStruct((...  6.84 us
  transfers between devices with their start and end apart: 25, of which 7 were waited for; matrix products, arithmetic and copies ran while one was open for 11% of the time, Pallas kernels for 4%

profile of v2, /device:TPU:8, one launch (start us, length us, event | category | flops | bytes accessed | tf_op | source)
XLA Modules:
  0.0 206.4 jit_solution(14317512719882637669)
XLA Ops:
  0.6 2.1 %head.1 = (bf16[2,136,1024]{2,1,0:T(8,128)(2,1)}, bf16[136,1024]{1,0:T(8,128)(2,1)}, s32[6,128]{1,0:T(8,128)}) custom-call(s32[6,128]{1,0:T(8,128)} %bitcast.85, bf16[6,128]{1,0:T(8,128)(2,1)} %bitcast.87, bf16[128,2048]{1,0:T(8,128)(2,1)} %tokens_ref.1), custom_call_target="tpu_custom_call" | custom-call | tf_op jit(solution)/shard_map/head/pallas_call | solution.py:165
  2.8 1.9 collective-permute-start
  4.7 1.7 collective-permute-done
  7.1 4.5 %collective-permute-start.3 = (bf16[2,136,1024]{2,1,0:T(8,128)(2,1)}, bf16[2,136,1024]{2,1,0:T(8,128)(2,1)S(1)}, u32[]{:S(2)}, u32[]{:S(2)}) collective-permute-start(bf16[2,136,1024]{2,1,0:T(8,128)(2,1)} %bitcast_dynamic-update-slice_fusion.refs_0_), channel_id=1, source_target_pairs={{0,16},{1,17},{2,18},{3,19},{4,20},{5,21},{6,22},{7,23},{8,24},{9,... | collective-permute-start | bytes 1671176 | tf_op jit(solution)/shard_map/ppermute | solution.py:36
  11.6 3.5 %collective-permute-start.4 = (bf16[2,136,1024]{2,1,0:T(8,128)(2,1)}, bf16[2,136,1024]{2,1,0:T(8,128)(2,1)S(1)}, u32[]{:S(2)}, u32[]{:S(2)}) collective-permute-start(bf16[2,136,1024]{2,1,0:T(8,128)(2,1)} %bitcast_dynamic-update-slice_fusion.refs_0_), channel_id=1, source_target_pairs={{0,48},{1,49},{2,50},{3,51},{4,52},{5,53},{6,54},{7,55},{8,56},{9,... | collective-permute-start | bytes 1671176 | tf_op jit(solution)/shard_map/ppermute | solution.py:36
  15.1 5.0 %collective-permute-start.1 = (bf16[2,136,1024]{2,1,0:T(8,128)(2,1)}, bf16[2,136,1024]{2,1,0:T(8,128)(2,1)S(1)}, u32[]{:S(2)}, u32[]{:S(2)}) collective-permute-start(bf16[2,136,1024]{2,1,0:T(8,128)(2,1)} %bitcast_dynamic-update-slice_fusion.refs_0_), channel_id=1, source_target_pairs={{0,8},{1,9},{2,10},{3,11},{4,12},{5,13},{6,14},{7,15},{8,16},{9,17... | collective-permute-start | bytes 1671176 | tf_op jit(solution)/shard_map/ppermute | solution.py:36
  20.1 4.6 %collective-permute-start.2 = (bf16[2,136,1024]{2,1,0:T(8,128)(2,1)}, bf16[2,136,1024]{2,1,0:T(8,128)(2,1)S(1)}, u32[]{:S(2)}, u32[]{:S(2)}) collective-permute-start(bf16[2,136,1024]{2,1,0:T(8,128)(2,1)} %bitcast_dynamic-update-slice_fusion.refs_0_), channel_id=1, source_target_pairs={{0,56},{1,57},{2,58},{3,59},{4,60},{5,61},{6,62},{7,63},{8,0},{9,1... | collective-permute-start | bytes 1671176 | tf_op jit(solution)/shard_map/ppermute | solution.py:36
  24.8 5.5 %collective-permute-start.5 = (bf16[2,136,1024]{2,1,0:T(8,128)(2,1)S(1)}, bf16[2,136,1024]{2,1,0:T(8,128)(2,1)S(1)}, u32[]{:S(2)}, u32[]{:S(2)}) collective-permute-start(bf16[2,136,1024]{2,1,0:T(8,128)(2,1)S(1)} %collective-permute-done.3.refs_3_), channel_id=1, source_target_pairs={{0,8},{1,9},{2,10},{3,11},{4,12},{5,13},{6,14},{7,15},{8,16},{9,17... | collective-permute-start | bytes 1671176 | tf_op jit(solution)/shard_map/ppermute | solution.py:36
  30.3 4.5 %collective-permute-start.7 = (bf16[2,136,1024]{2,1,0:T(8,128)(2,1)S(1)}, bf16[2,136,1024]{2,1,0:T(8,128)(2,1)S(1)}, u32[]{:S(2)}, u32[]{:S(2)}) collective-permute-start(bf16[2,136,1024]{2,1,0:T(8,128)(2,1)S(1)} %collective-permute-done.3.refs_3_), channel_id=1, source_target_pairs={{0,16},{1,17},{2,18},{3,19},{4,20},{5,21},{6,22},{7,23},{8,24},{9,... | collective-permute-start | bytes 1671176 | tf_op jit(solution)/shard_map/ppermute | solution.py:36
  34.8 2.1 %collective-permute-start.6 = (bf16[2,136,1024]{2,1,0:T(8,128)(2,1)S(1)}, bf16[2,136,1024]{2,1,0:T(8,128)(2,1)}, u32[]{:S(2)}, u32[]{:S(2)}) collective-permute-start(bf16[2,136,1024]{2,1,0:T(8,128)(2,1)S(1)} %collective-permute-done.4.refs_4_), channel_id=1, source_target_pairs={{0,56},{1,57},{2,58},{3,59},{4,60},{5,61},{6,62},{7,63},{8,0},{9,1... | collective-permute-start | bytes 1671176 | tf_op jit(solution)/shard_map/ppermute | solution.py:36
  37.0 1.2 compare_select_fusion.8.place_ref
  38.2 2.4 %collective-permute-done.5.refs_5_ = bf16[2,136,1024]{2,1,0:T(8,128)(2,1)S(1)} collective-permute-done((bf16[2,136,1024]{2,1,0:T(8,128)(2,1)S(1)}, bf16[2,136,1024]{2,1,0:T(8,128)(2,1)S(1)}, u32[]{:S(2)}, u32[]{:S(2)}) %collective-permute-start.5) | collective-permute-done | bytes 557088 | tf_op jit(solution)/shard_map/ppermute | solution.py:36
  40.5 14.6 %collective-permute-done.7.refs_7_ = bf16[2,136,1024]{2,1,0:T(8,128)(2,1)S(1)} collective-permute-done((bf16[2,136,1024]{2,1,0:T(8,128)(2,1)S(1)}, bf16[2,136,1024]{2,1,0:T(8,128)(2,1)S(1)}, u32[]{:S(2)}, u32[]{:S(2)}) %collective-permute-start.7) | collective-permute-done | bytes 557088 | tf_op jit(solution)/shard_map/ppermute | solution.py:36
  56.0 5.7 %route.1 = (bf16[272,1024]{1,0:T(8,128)(2,1)}, bf16[272,1024]{1,0:T(8,128)(2,1)}, bf16[272,1024]{1,0:T(8,128)(2,1)}, bf16[272,1024]{1,0:T(8,128)(2,1)}, bf16[272...) custom-call(s32[11]{0:T(128)} %compare_select_fusion.8.place_ref, ...), custom_call_target="tpu_custom_call" | custom-call | tf_op jit(solution)/shard_map/route/pallas_call | solution.py:190
  61.6 6.5 %collective-permute-start.11 = (bf16[272,1024]{1,0:T(8,128)(2,1)}, bf16[272,1024]{1,0:T(8,128)(2,1)S(1)}, u32[]{:S(2)}, u32[]{:S(2)}) collective-permute-start(bf16[272,1024]{1,0:T(8,128)(2,1)} %get-tuple-element.23), channel_id=1, source_target_pairs={{0,4},{1,5},{2,6},{3,7},{4,0},{5,1},{6,2},{7,3},{8,12},{9,13},{10,... | collective-permute-start | bytes 1671176 | tf_op jit(solution)/shard_map/ppermute | solution.py:36
  68.2 3.4 %collective-permute-start.8 = (bf16[272,1024]{1,0:T(8,128)(2,1)}, bf16[272,1024]{1,0:T(8,128)(2,1)S(1)}, u32[]{:S(2)}, u32[]{:S(2)}) collective-permute-start(bf16[272,1024]{1,0:T(8,128)(2,1)} %get-tuple-element.20), channel_id=1, source_target_pairs={{0,1},{1,2},{2,3},{3,4},{4,5},{5,6},{6,7},{7,0},{8,9},{9,10},{10,1... | collective-permute-start | bytes 1671176 | tf_op jit(solution)/shard_map/ppermute | solution.py:36
  71.5 3.7 %collective-permute-start.14 = (bf16[272,1024]{1,0:T(8,128)(2,1)}, bf16[272,1024]{1,0:T(8,128)(2,1)S(1)}, u32[]{:S(2)}, u32[]{:S(2)}) collective-permute-start(bf16[272,1024]{1,0:T(8,128)(2,1)} %get-tuple-element.26), channel_id=1, source_target_pairs={{0,7},{1,0},{2,1},{3,2},{4,3},{5,4},{6,5},{7,6},{8,15},{9,8},{10,9... | collective-permute-start | bytes 1671176 | tf_op jit(solution)/shard_map/ppermute | solution.py:36
  75.2 1.7 bitcast_dynamic-update-slice_fusion.1
  77.0 4.0 %collective-permute-start.10 = (bf16[272,1024]{1,0:T(8,128)(2,1)}, bf16[272,1024]{1,0:T(8,128)(2,1)S(1)}, u32[]{:S(2)}, u32[]{:S(2)}) collective-permute-start(bf16[272,1024]{1,0:T(8,128)(2,1)} %get-tuple-element.22), channel_id=1, source_target_pairs={{0,3},{1,4},{2,5},{3,6},{4,7},{5,0},{6,1},{7,2},{8,11},{9,12},{10,... | collective-permute-start | bytes 1671176 | tf_op jit(solution)/shard_map/ppermute | solution.py:36
  81.0 4.9 %collective-permute-start.12 = (bf16[272,1024]{1,0:T(8,128)(2,1)}, bf16[272,1024]{1,0:T(8,128)(2,1)S(1)}, u32[]{:S(2)}, u32[]{:S(2)}) collective-permute-start(bf16[272,1024]{1,0:T(8,128)(2,1)} %get-tuple-element.24), channel_id=1, source_target_pairs={{0,5},{1,6},{2,7},{3,0},{4,1},{5,2},{6,3},{7,4},{8,13},{9,14},{10,... | collective-permute-start | bytes 1671176 | tf_op jit(solution)/shard_map/ppermute | solution.py:36
  85.9 3.1 %collective-permute-start.9 = (bf16[272,1024]{1,0:T(8,128)(2,1)}, bf16[272,1024]{1,0:T(8,128)(2,1)S(1)}, u32[]{:S(2)}, u32[]{:S(2)}) collective-permute-start(bf16[272,1024]{1,0:T(8,128)(2,1)} %get-tuple-element.21), channel_id=1, source_target_pairs={{0,2},{1,3},{2,4},{3,5},{4,6},{5,7},{6,0},{7,1},{8,10},{9,11},{10,... | collective-permute-start | bytes 1671176 | tf_op jit(solution)/shard_map/ppermute | solution.py:36
  91.3 19.9 %collective-permute-done.10.refs_3_ = bf16[272,1024]{1,0:T(8,128)(2,1)S(1)} collective-permute-done((bf16[272,1024]{1,0:T(8,128)(2,1)}, bf16[272,1024]{1,0:T(8,128)(2,1)S(1)}, u32[]{:S(2)}, u32[]{:S(2)}) %collective-permute-start.10) | collective-permute-done | bytes 557088 | tf_op jit(solution)/shard_map/ppermute | solution.py:36
  112.7 1.9 collective-permute-start.15
  114.6 2.1 collective-permute-start.13
  116.7 4.9 %collective-permute-start.17 = (bf16[256,704]{0,1:T(8,128)(2,1)S(1)}, bf16[256,704]{0,1:T(8,128)(2,1)S(1)}, u32[]{:S(2)}, u32[]{:S(2)}) collective-permute-start(bf16[256,704]{0,1:T(8,128)(2,1)S(1)} %bitcast.77), channel_id=1, source_target_pairs={{0,384},{64,448},{128,0},{192,64},{256,128},{320,192},{384,256},{4... | collective-permute-start | bytes 1081352 | tf_op jit(solution)/shard_map/ppermute | solution.py:22
  121.6 2.7 %collective-permute-start.18 = (bf16[256,704]{0,1:T(8,128)(2,1)S(1)}, bf16[256,704]{0,1:T(8,128)(2,1)S(1)}, u32[]{:S(2)}, u32[]{:S(2)}) collective-permute-start(bf16[256,704]{0,1:T(8,128)(2,1)S(1)} %bitcast.78), channel_id=1, source_target_pairs={{0,256},{64,320},{128,384},{192,448},{256,0},{320,64},{384,128},{4... | collective-permute-start | bytes 1081352 | tf_op jit(solution)/shard_map/ppermute | solution.py:22
  124.4 2.8 %collective-permute-start.19 = (bf16[256,704]{0,1:T(8,128)(2,1)S(1)}, bf16[256,704]{0,1:T(8,128)(2,1)S(1)}, u32[]{:S(2)}, u32[]{:S(2)}) collective-permute-start(bf16[256,704]{0,1:T(8,128)(2,1)S(1)} %bitcast.79), channel_id=1, source_target_pairs={{0,128},{64,192},{128,256},{192,320},{256,384},{320,448},{384,0},{... | collective-permute-start | bytes 1081352 | tf_op jit(solution)/shard_map/ppermute | solution.py:22
  127.3 3.1 %collective-permute-done.13.refs_6_ = bf16[272,1024]{1,0:T(8,128)(2,1)S(1)} collective-permute-done((bf16[272,1024]{1,0:T(8,128)(2,1)S(1)}, bf16[272,1024]{1,0:T(8,128)(2,1)S(1)}, u32[]{:S(2)}, u32[]{:S(2)}) %collective-permute-start.13) | collective-permute-done | bytes 557088 | tf_op jit(solution)/shard_map/ppermute | solution.py:36
  130.4 0.9 pad_maximum_fusion.1
  131.3 4.2 %collective-permute-start.16 = (bf16[2,128,1024]{2,1,0:T(8,128)(2,1)}, bf16[2,128,1024]{2,1,0:T(8,128)(2,1)}, u32[]{:S(2)}, u32[]{:S(2)}) collective-permute-start(bf16[2,128,1024]{2,1,0:T(8,128)(2,1)} %pad_maximum_fusion.1), channel_id=1, source_target_pairs={{0,64},{64,0},{128,192},{192,128},{256,320},{320,256},{384,448},{4... | collective-permute-start | bytes 1572872 | tf_op jit(solution)/shard_map/ppermute | solution.py:26
  135.5 1.7 collective-permute-done.17
  137.2 6.8 %collective-permute-done.19 = bf16[256,704]{0,1:T(8,128)(2,1)S(1)} collective-permute-done((bf16[256,704]{0,1:T(8,128)(2,1)S(1)}, bf16[256,704]{0,1:T(8,128)(2,1)S(1)}, u32[]{:S(2)}, u32[]{:S(2)}) %collective-permute-start.19) | collective-permute-done | bytes 360480 | tf_op jit(solution)/shard_map/ppermute | solution.py:22
  144.1 1.3 pad_maximum_fusion
  145.3 2.0 collective-permute-start.20
  148.2 6.8 %join.1 = (bf16[1024,2048]{1,0:T(8,128)(2,1)}, bf16[1024,2048]{1,0:T(8,128)(2,1)}, bf16[1024,128]{1,0:T(8,128)(2,1)}) custom-call(s32[2,64]{1,0:T(2,128)} %pad_add_fusion.slots_ref, bf16[272,1024]{1,0:T(8,128)(2,1)} %get-tuple-element.19.refs_0_, bf16[272,1024]{1,0:T(8,128)(2,1)} %copy-done.8, bf16[272,1024]{1,0:T(8,128)(2,1)} %copy-done.12, ...), custom_call_target="tpu_custom_call" | custom-call | tf_op jit(solution)/shard_map/join/pallas_call | solution.py:206
  155.1 3.7 %fusion.10 = bf16[1024,704]{0,1:T(8,128)(2,1)S(1)} fusion(bf16[1024,704]{0,1:T(8,128)(2,1)} %param.9, bf16[1024,2048]{1,0:T(8,128)(2,1)} %get-tuple-element.29), kind=kOutput, calls=%fused_computation.9 | convolution fusion | flops 1477115904 | bytes 4980736 | tf_op jit(solution)/shard_map/dot_general | solution.py:222
  158.9 2.4 %collective-permute-start.21 = (bf16[4,256,704]{1,2,0:T(8,128)(2,1)S(1)}, bf16[4,256,704]{1,2,0:T(8,128)(2,1)S(1)}, u32[]{:S(2)}, u32[]{:S(2)}) collective-permute-start(bf16[4,256,704]{1,2,0:T(8,128)(2,1)S(1)} %bitcast.75), channel_id=1, source_target_pairs={{0,64},{64,0},{128,192},{192,128},{256,320},{320,256},{384,448},{4... | collective-permute-start | bytes 4325384 | tf_op jit(solution)/shard_map/ppermute | solution.py:26
  161.5 1.5 constant_dynamic-update-slice_fusion
  164.1 1.2 copy-done.22
  165.7 1.7 fusion.7
  167.9 1.0 slice_bitcast_fusion.3
  168.9 2.8 %collective-permute-start.22 = (bf16[256,704]{0,1:T(8,128)(2,1)}, bf16[256,704]{0,1:T(8,128)(2,1)S(1)}, u32[]{:S(2)}, u32[]{:S(2)}) collective-permute-start(bf16[256,704]{0,1:T(8,128)(2,1)} %get-tuple-element.35), channel_id=1, source_target_pairs={{0,256},{64,320},{128,384},{192,448},{256,0},{320,64},{384,128},{4... | collective-permute-start | bytes 1081352 | tf_op jit(solution)/shard_map/ppermute | solution.py:22
  171.7 2.1 collective-permute-start.23
  173.8 5.0 %collective-permute-start.24 = (bf16[256,704]{0,1:T(8,128)(2,1)}, bf16[256,704]{0,1:T(8,128)(2,1)}, u32[]{:S(2)}, u32[]{:S(2)}) collective-permute-start(bf16[256,704]{0,1:T(8,128)(2,1)} %get-tuple-element.36), channel_id=1, source_target_pairs={{0,384},{64,448},{128,0},{192,64},{256,128},{320,192},{384,256},{4... | collective-permute-start | bytes 1081352 | tf_op jit(solution)/shard_map/ppermute | solution.py:22
  178.8 4.4 %multiply_reduce_fusion = (f32[1024]{0:T(1024)S(1)}, bf16[1024,704]{0,1:T(8,128)(2,1)}) fusion(bf16[1024,704]{0,1:T(8,128)(2,1)S(1)} %copy-done.23, f32[1024]{0:T(1024)S(1)} %convert_reduce_fusion, bf16[1024,2048]{1,0:T(8,128)(2,1)S(1)} %copy-done.21, bf16[2048,704]{0,1:T(8,128)(2,1)S(1)} %bitcast.73), kind=kOutput, calls=%fused_computation.1 | convolution fusion | flops 2956393472 | bytes 9969664 | tf_op jit(solution)/shard_map/dot_general | solution.py:233
  183.3 19.3 %all_to_all.11 = f32[64,1,16]{2,1,0:T(1,128)} all-to-all(f32[64,1,16]{2,1,0:T(1,128)S(1)} %bitcast.84), channel_id=1, replica_groups=mesh['dp'=8,'expert'=64] {'expert'}, dimensions={0} | all-to-all | bytes 8192 | tf_op jit(solution)/shard_map/all_to_all | solution.py:40
  202.6 1.6 pick.1
  204.3 2.1 %fusion.16 = f32[1,256,704]{1,2,0:T(8,128)} fusion(f32[4,256,704]{1,2,0:T(8,128)S(1)} %get-tuple-element.32, bf16[256,704]{0,1:T(8,128)(2,1)} %collective-permute-done.24, bf16[256,704]{0,1:T(8,128)(2,1)} %collective-permute-done.23, bf16[256,704]{0,1:T(8,128)(2,1)S(1)} %collective-permute-done.22), kind=kLoop, calls=%fused_computation.16 | loop fusion | flops 1081344 | bytes 2523136 | tf_op jit(solution)/shard_map/broadcast_in_dim | solution.py:239
  (90 shorter events, 8.6 us)
Async XLA Ops:
  2.8 3.7 %collective-permute-start = (bf16[136,1024]{1,0:T(8,128)(2,1)}, bf16[136,1024]{1,0:T(8,128)(2,1)S(1)}, u32[]{:S(2)}, u32[]{:S(2)}) collective-permute-start(bf16[136,1024]{1,0:T(8,128)(2,1)} %get-tuple-element.18), channel_id=1, source_target_pairs={{0,64},{64,0},{128,192},{192,128},{256,320},{320,256},{384,448},{4... | collective-permute-start | bytes 835592 | tf_op jit(solution)/shard_map/ppermute | solution.py:26
  7.1 17.6 %collective-permute-start.3 = (bf16[2,136,1024]{2,1,0:T(8,128)(2,1)}, bf16[2,136,1024]{2,1,0:T(8,128)(2,1)S(1)}, u32[]{:S(2)}, u32[]{:S(2)}) collective-permute-start(bf16[2,136,1024]{2,1,0:T(8,128)(2,1)} %bitcast_dynamic-update-slice_fusion.refs_0_), channel_id=1, source_target_pairs={{0,16},{1,17},{2,18},{3,19},{4,20},{5,21},{6,22},{7,23},{8,24},{9,... | collective-permute-start | bytes 1671176 | tf_op jit(solution)/shard_map/ppermute | solution.py:36
  11.6 23.2 %collective-permute-start.4 = (bf16[2,136,1024]{2,1,0:T(8,128)(2,1)}, bf16[2,136,1024]{2,1,0:T(8,128)(2,1)S(1)}, u32[]{:S(2)}, u32[]{:S(2)}) collective-permute-start(bf16[2,136,1024]{2,1,0:T(8,128)(2,1)} %bitcast_dynamic-update-slice_fusion.refs_0_), channel_id=1, source_target_pairs={{0,48},{1,49},{2,50},{3,51},{4,52},{5,53},{6,54},{7,55},{8,56},{9,... | collective-permute-start | bytes 1671176 | tf_op jit(solution)/shard_map/ppermute | solution.py:36
  15.1 23.1 %collective-permute-start.1 = (bf16[2,136,1024]{2,1,0:T(8,128)(2,1)}, bf16[2,136,1024]{2,1,0:T(8,128)(2,1)S(1)}, u32[]{:S(2)}, u32[]{:S(2)}) collective-permute-start(bf16[2,136,1024]{2,1,0:T(8,128)(2,1)} %bitcast_dynamic-update-slice_fusion.refs_0_), channel_id=1, source_target_pairs={{0,8},{1,9},{2,10},{3,11},{4,12},{5,13},{6,14},{7,15},{8,16},{9,17... | collective-permute-start | bytes 1671176 | tf_op jit(solution)/shard_map/ppermute | solution.py:36
  20.1 18.0 %collective-permute-start.2 = (bf16[2,136,1024]{2,1,0:T(8,128)(2,1)}, bf16[2,136,1024]{2,1,0:T(8,128)(2,1)S(1)}, u32[]{:S(2)}, u32[]{:S(2)}) collective-permute-start(bf16[2,136,1024]{2,1,0:T(8,128)(2,1)} %bitcast_dynamic-update-slice_fusion.refs_0_), channel_id=1, source_target_pairs={{0,56},{1,57},{2,58},{3,59},{4,60},{5,61},{6,62},{7,63},{8,0},{9,1... | collective-permute-start | bytes 1671176 | tf_op jit(solution)/shard_map/ppermute | solution.py:36
  24.7 30.4 %copy-start.14 = (bf16[2,136,1024]{2,1,0:T(8,128)(2,1)}, bf16[2,136,1024]{2,1,0:T(8,128)(2,1)S(1)}, u32[]{:S(2)}) copy-start(bf16[2,136,1024]{2,1,0:T(8,128)(2,1)S(1)} %collective-permute-done.3.refs_3_) | copy-start | bytes 1671172
  24.8 15.8 %collective-permute-start.5 = (bf16[2,136,1024]{2,1,0:T(8,128)(2,1)S(1)}, bf16[2,136,1024]{2,1,0:T(8,128)(2,1)S(1)}, u32[]{:S(2)}, u32[]{:S(2)}) collective-permute-start(bf16[2,136,1024]{2,1,0:T(8,128)(2,1)S(1)} %collective-permute-done.3.refs_3_), channel_id=1, source_target_pairs={{0,8},{1,9},{2,10},{3,11},{4,12},{5,13},{6,14},{7,15},{8,16},{9,17... | collective-permute-start | bytes 1671176 | tf_op jit(solution)/shard_map/ppermute | solution.py:36
  30.3 24.8 %collective-permute-start.7 = (bf16[2,136,1024]{2,1,0:T(8,128)(2,1)S(1)}, bf16[2,136,1024]{2,1,0:T(8,128)(2,1)S(1)}, u32[]{:S(2)}, u32[]{:S(2)}) collective-permute-start(bf16[2,136,1024]{2,1,0:T(8,128)(2,1)S(1)} %collective-permute-done.3.refs_3_), channel_id=1, source_target_pairs={{0,16},{1,17},{2,18},{3,19},{4,20},{5,21},{6,22},{7,23},{8,24},{9,... | collective-permute-start | bytes 1671176 | tf_op jit(solution)/shard_map/ppermute | solution.py:36
  34.8 20.3 %copy-start.15 = (bf16[2,136,1024]{2,1,0:T(8,128)(2,1)}, bf16[2,136,1024]{2,1,0:T(8,128)(2,1)S(1)}, u32[]{:S(2)}) copy-start(bf16[2,136,1024]{2,1,0:T(8,128)(2,1)S(1)} %collective-permute-done.4.refs_4_) | copy-start | bytes 1671172
  34.8 20.3 %collective-permute-start.6 = (bf16[2,136,1024]{2,1,0:T(8,128)(2,1)S(1)}, bf16[2,136,1024]{2,1,0:T(8,128)(2,1)}, u32[]{:S(2)}, u32[]{:S(2)}) collective-permute-start(bf16[2,136,1024]{2,1,0:T(8,128)(2,1)S(1)} %collective-permute-done.4.refs_4_), channel_id=1, source_target_pairs={{0,56},{1,57},{2,58},{3,59},{4,60},{5,61},{6,62},{7,63},{8,0},{9,1... | collective-permute-start | bytes 1671176 | tf_op jit(solution)/shard_map/ppermute | solution.py:36
  38.1 17.0 %copy-start.16 = (bf16[2,136,1024]{2,1,0:T(8,128)(2,1)}, bf16[2,136,1024]{2,1,0:T(8,128)(2,1)S(1)}, u32[]{:S(2)}) copy-start(bf16[2,136,1024]{2,1,0:T(8,128)(2,1)S(1)} %collective-permute-done.1.refs_1_) | copy-start | bytes 1671172
  38.2 17.0 %copy-start.17 = (bf16[2,136,1024]{2,1,0:T(8,128)(2,1)}, bf16[2,136,1024]{2,1,0:T(8,128)(2,1)S(1)}, u32[]{:S(2)}) copy-start(bf16[2,136,1024]{2,1,0:T(8,128)(2,1)S(1)} %collective-permute-done.2.refs_2_) | copy-start | bytes 1671172
  40.5 14.6 %copy-start.18 = (bf16[2,136,1024]{2,1,0:T(8,128)(2,1)}, bf16[2,136,1024]{2,1,0:T(8,128)(2,1)S(1)}, u32[]{:S(2)}) copy-start(bf16[2,136,1024]{2,1,0:T(8,128)(2,1)S(1)} %collective-permute-done.5.refs_5_) | copy-start | bytes 1671172
  61.6 24.2 %collective-permute-start.11 = (bf16[272,1024]{1,0:T(8,128)(2,1)}, bf16[272,1024]{1,0:T(8,128)(2,1)S(1)}, u32[]{:S(2)}, u32[]{:S(2)}) collective-permute-start(bf16[272,1024]{1,0:T(8,128)(2,1)} %get-tuple-element.23), channel_id=1, source_target_pairs={{0,4},{1,5},{2,6},{3,7},{4,0},{5,1},{6,2},{7,3},{8,12},{9,13},{10,... | collective-permute-start | bytes 1671176 | tf_op jit(solution)/shard_map/ppermute | solution.py:36
  68.2 21.5 %collective-permute-start.8 = (bf16[272,1024]{1,0:T(8,128)(2,1)}, bf16[272,1024]{1,0:T(8,128)(2,1)S(1)}, u32[]{:S(2)}, u32[]{:S(2)}) collective-permute-start(bf16[272,1024]{1,0:T(8,128)(2,1)} %get-tuple-element.20), channel_id=1, source_target_pairs={{0,1},{1,2},{2,3},{3,4},{4,5},{5,6},{6,7},{7,0},{8,9},{9,10},{10,1... | collective-permute-start | bytes 1671176 | tf_op jit(solution)/shard_map/ppermute | solution.py:36
  71.5 18.9 %collective-permute-start.14 = (bf16[272,1024]{1,0:T(8,128)(2,1)}, bf16[272,1024]{1,0:T(8,128)(2,1)S(1)}, u32[]{:S(2)}, u32[]{:S(2)}) collective-permute-start(bf16[272,1024]{1,0:T(8,128)(2,1)} %get-tuple-element.26), channel_id=1, source_target_pairs={{0,7},{1,0},{2,1},{3,2},{4,3},{5,4},{6,5},{7,6},{8,15},{9,8},{10,9... | collective-permute-start | bytes 1671176 | tf_op jit(solution)/shard_map/ppermute | solution.py:36
  75.2 39.4 %copy-start.24 = (bf16[272,1024]{1,0:T(8,128)(2,1)S(1)}, bf16[272,1024]{1,0:T(8,128)(2,1)}, u32[]{:S(2)}) copy-start(bf16[272,1024]{1,0:T(8,128)(2,1)} %get-tuple-element.25) | copy-start | bytes 1671172
  75.2 41.5 %copy-start = (bf16[1,256,704]{1,2,0:T(8,128)(2,1)S(1)}, bf16[1,256,704]{1,2,0:T(8,128)(2,1)}, u32[]{:S(2)}) copy-start(bf16[1,256,704]{1,2,0:T(8,128)(2,1)} %param.10) | copy-start | bytes 1081348
  77.0 34.2 %collective-permute-start.10 = (bf16[272,1024]{1,0:T(8,128)(2,1)}, bf16[272,1024]{1,0:T(8,128)(2,1)S(1)}, u32[]{:S(2)}, u32[]{:S(2)}) collective-permute-start(bf16[272,1024]{1,0:T(8,128)(2,1)} %get-tuple-element.22), channel_id=1, source_target_pairs={{0,3},{1,4},{2,5},{3,6},{4,7},{5,0},{6,1},{7,2},{8,11},{9,12},{10,... | collective-permute-start | bytes 1671176 | tf_op jit(solution)/shard_map/ppermute | solution.py:36
  81.0 30.9 %collective-permute-start.12 = (bf16[272,1024]{1,0:T(8,128)(2,1)}, bf16[272,1024]{1,0:T(8,128)(2,1)S(1)}, u32[]{:S(2)}, u32[]{:S(2)}) collective-permute-start(bf16[272,1024]{1,0:T(8,128)(2,1)} %get-tuple-element.24), channel_id=1, source_target_pairs={{0,5},{1,6},{2,7},{3,0},{4,1},{5,2},{6,3},{7,4},{8,13},{9,14},{10,... | collective-permute-start | bytes 1671176 | tf_op jit(solution)/shard_map/ppermute | solution.py:36
  85.9 41.4 %copy-start.7 = (bf16[272,1024]{1,0:T(8,128)(2,1)}, bf16[272,1024]{1,0:T(8,128)(2,1)S(1)}, u32[]{:S(2)}) copy-start(bf16[272,1024]{1,0:T(8,128)(2,1)S(1)} %collective-permute-done.11.refs_4_) | copy-start | bytes 1671172
  85.9 38.5 %collective-permute-start.9 = (bf16[272,1024]{1,0:T(8,128)(2,1)}, bf16[272,1024]{1,0:T(8,128)(2,1)S(1)}, u32[]{:S(2)}, u32[]{:S(2)}) collective-permute-start(bf16[272,1024]{1,0:T(8,128)(2,1)} %get-tuple-element.21), channel_id=1, source_target_pairs={{0,2},{1,3},{2,4},{3,5},{4,6},{5,7},{6,0},{7,1},{8,10},{9,11},{10,... | collective-permute-start | bytes 1671176 | tf_op jit(solution)/shard_map/ppermute | solution.py:36
  89.7 40.7 %copy-start.8 = (bf16[272,1024]{1,0:T(8,128)(2,1)}, bf16[272,1024]{1,0:T(8,128)(2,1)S(1)}, u32[]{:S(2)}) copy-start(bf16[272,1024]{1,0:T(8,128)(2,1)S(1)} %collective-permute-done.8.refs_1_) | copy-start | bytes 1671172
  90.5 39.9 %copy-start.9 = (bf16[272,1024]{1,0:T(8,128)(2,1)}, bf16[272,1024]{1,0:T(8,128)(2,1)S(1)}, u32[]{:S(2)}) copy-start(bf16[272,1024]{1,0:T(8,128)(2,1)S(1)} %collective-permute-done.14.refs_7_) | copy-start | bytes 1671172
  111.2 20.1 %copy-start.10 = (bf16[272,1024]{1,0:T(8,128)(2,1)}, bf16[272,1024]{1,0:T(8,128)(2,1)S(1)}, u32[]{:S(2)}) copy-start(bf16[272,1024]{1,0:T(8,128)(2,1)S(1)} %collective-permute-done.10.refs_3_) | copy-start | bytes 1671172
  111.9 32.1 %copy-start.11 = (bf16[272,1024]{1,0:T(8,128)(2,1)}, bf16[272,1024]{1,0:T(8,128)(2,1)S(1)}, u32[]{:S(2)}) copy-start(bf16[272,1024]{1,0:T(8,128)(2,1)S(1)} %collective-permute-done.12.refs_5_) | copy-start | bytes 1671172
  112.7 35.5 %collective-permute-start.15 = (bf16[6,128,1024]{2,1,0:T(8,128)(2,1)}, bf16[6,128,1024]{2,1,0:T(8,128)(2,1)}, u32[]{:S(2)}, u32[]{:S(2)}) collective-permute-start(bf16[6,128,1024]{2,1,0:T(8,128)(2,1)} %fusion.17), channel_id=1, source_target_pairs={{0,64},{64,0},{128,192},{192,128},{256,320},{320,256},{384,448},{4... | collective-permute-start | bytes 4718600 | tf_op jit(solution)/shard_map/ppermute | solution.py:26
  114.6 15.7 %collective-permute-start.13 = (bf16[272,1024]{1,0:T(8,128)(2,1)S(1)}, bf16[272,1024]{1,0:T(8,128)(2,1)S(1)}, u32[]{:S(2)}, u32[]{:S(2)}) collective-permute-start(bf16[272,1024]{1,0:T(8,128)(2,1)S(1)} %copy-done.24), channel_id=1, source_target_pairs={{0,6},{1,7},{2,0},{3,1},{4,2},{5,3},{6,4},{7,5},{8,14},{9,15},{10,... | collective-permute-start | bytes 1671176 | tf_op jit(solution)/shard_map/ppermute | solution.py:36
  116.7 20.5 %collective-permute-start.17 = (bf16[256,704]{0,1:T(8,128)(2,1)S(1)}, bf16[256,704]{0,1:T(8,128)(2,1)S(1)}, u32[]{:S(2)}, u32[]{:S(2)}) collective-permute-start(bf16[256,704]{0,1:T(8,128)(2,1)S(1)} %bitcast.77), channel_id=1, source_target_pairs={{0,384},{64,448},{128,0},{192,64},{256,128},{320,192},{384,256},{4... | collective-permute-start | bytes 1081352 | tf_op jit(solution)/shard_map/ppermute | solution.py:22
  121.6 15.5 %collective-permute-start.18 = (bf16[256,704]{0,1:T(8,128)(2,1)S(1)}, bf16[256,704]{0,1:T(8,128)(2,1)S(1)}, u32[]{:S(2)}, u32[]{:S(2)}) collective-permute-start(bf16[256,704]{0,1:T(8,128)(2,1)S(1)} %bitcast.78), channel_id=1, source_target_pairs={{0,256},{64,320},{128,384},{192,448},{256,0},{320,64},{384,128},{4... | collective-permute-start | bytes 1081352 | tf_op jit(solution)/shard_map/ppermute | solution.py:22
  124.4 19.6 %copy-start.12 = (bf16[272,1024]{1,0:T(8,128)(2,1)}, bf16[272,1024]{1,0:T(8,128)(2,1)S(1)}, u32[]{:S(2)}) copy-start(bf16[272,1024]{1,0:T(8,128)(2,1)S(1)} %collective-permute-done.9.refs_2_) | copy-start | bytes 1671172
  124.4 19.6 %collective-permute-start.19 = (bf16[256,704]{0,1:T(8,128)(2,1)S(1)}, bf16[256,704]{0,1:T(8,128)(2,1)S(1)}, u32[]{:S(2)}, u32[]{:S(2)}) collective-permute-start(bf16[256,704]{0,1:T(8,128)(2,1)S(1)} %bitcast.79), channel_id=1, source_target_pairs={{0,128},{64,192},{128,256},{192,320},{256,384},{320,448},{384,0},{... | collective-permute-start | bytes 1081352 | tf_op jit(solution)/shard_map/ppermute | solution.py:22
  130.3 13.7 %copy-start.13 = (bf16[272,1024]{1,0:T(8,128)(2,1)}, bf16[272,1024]{1,0:T(8,128)(2,1)S(1)}, u32[]{:S(2)}) copy-start(bf16[272,1024]{1,0:T(8,128)(2,1)S(1)} %collective-permute-done.13.refs_6_) | copy-start | bytes 1671172
  131.3 17.0 %collective-permute-start.16 = (bf16[2,128,1024]{2,1,0:T(8,128)(2,1)}, bf16[2,128,1024]{2,1,0:T(8,128)(2,1)}, u32[]{:S(2)}, u32[]{:S(2)}) collective-permute-start(bf16[2,128,1024]{2,1,0:T(8,128)(2,1)} %pad_maximum_fusion.1), channel_id=1, source_target_pairs={{0,64},{64,0},{128,192},{192,128},{256,320},{320,256},{384,448},{4... | collective-permute-start | bytes 1572872 | tf_op jit(solution)/shard_map/ppermute | solution.py:26
  137.2 6.9 %copy-start.1 = (bf16[256,704]{0,1:T(8,128)(2,1)}, bf16[256,704]{0,1:T(8,128)(2,1)S(1)}, u32[]{:S(2)}) copy-start(bf16[256,704]{0,1:T(8,128)(2,1)S(1)} %collective-permute-done.17) | copy-start | bytes 1081348
  137.2 8.1 %copy-start.3 = (bf16[256,704]{0,1:T(8,128)(2,1)}, bf16[256,704]{0,1:T(8,128)(2,1)S(1)}, u32[]{:S(2)}) copy-start(bf16[256,704]{0,1:T(8,128)(2,1)S(1)} %collective-permute-done.18) | copy-start | bytes 1081348
  144.0 3.3 %copy-start.5 = (bf16[256,704]{0,1:T(8,128)(2,1)}, bf16[256,704]{0,1:T(8,128)(2,1)S(1)}, u32[]{:S(2)}) copy-start(bf16[256,704]{0,1:T(8,128)(2,1)S(1)} %collective-permute-done.19) | copy-start | bytes 1081348
  145.3 16.1 %collective-permute-start.20 = (bf16[4,256,704]{1,2,0:T(8,128)(2,1)}, bf16[4,256,704]{1,2,0:T(8,128)(2,1)}, u32[]{:S(2)}, u32[]{:S(2)}) collective-permute-start(bf16[4,256,704]{1,2,0:T(8,128)(2,1)} %pad_maximum_fusion), channel_id=1, source_target_pairs={{0,64},{64,0},{128,192},{192,128},{256,320},{320,256},{384,448},{4... | collective-permute-start | bytes 4325384 | tf_op jit(solution)/shard_map/ppermute | solution.py:26
  158.8 2.6 %copy-start.2 = (bf16[256,704]{0,1:T(8,128)(2,1)S(1)}, bf16[256,704]{0,1:T(8,128)(2,1)}, u32[]{:S(2)}) copy-start(bf16[256,704]{0,1:T(8,128)(2,1)} %copy-done.1) | copy-start | bytes 1081348
  158.8 2.6 %copy-start.4 = (bf16[256,704]{0,1:T(8,128)(2,1)S(1)}, bf16[256,704]{0,1:T(8,128)(2,1)}, u32[]{:S(2)}) copy-start(bf16[256,704]{0,1:T(8,128)(2,1)} %copy-done.3) | copy-start | bytes 1081348
  158.8 2.6 %copy-start.6 = (bf16[256,704]{0,1:T(8,128)(2,1)S(1)}, bf16[256,704]{0,1:T(8,128)(2,1)}, u32[]{:S(2)}) copy-start(bf16[256,704]{0,1:T(8,128)(2,1)} %copy-done.5) | copy-start | bytes 1081348
  158.9 8.5 %collective-permute-start.21 = (bf16[4,256,704]{1,2,0:T(8,128)(2,1)S(1)}, bf16[4,256,704]{1,2,0:T(8,128)(2,1)S(1)}, u32[]{:S(2)}, u32[]{:S(2)}) collective-permute-start(bf16[4,256,704]{1,2,0:T(8,128)(2,1)S(1)} %bitcast.75), channel_id=1, source_target_pairs={{0,64},{64,0},{128,192},{192,128},{256,320},{320,256},{384,448},{4... | collective-permute-start | bytes 4325384 | tf_op jit(solution)/shard_map/ppermute | solution.py:26
  163.0 2.3 %copy-start.22 = (bf16[1024,2048]{1,0:T(8,128)(2,1)S(1)}, bf16[1024,2048]{1,0:T(8,128)(2,1)}, u32[]{:S(2)}) copy-start(bf16[1024,2048]{1,0:T(8,128)(2,1)} %get-tuple-element.29) | copy-start | bytes 12582916
  163.0 2.7 %copy-start.23 = (bf16[1024,704]{0,1:T(8,128)(2,1)S(1)}, bf16[1024,704]{0,1:T(8,128)(2,1)}, u32[]{:S(2)}) copy-start(bf16[1024,704]{0,1:T(8,128)(2,1)} %param.9) | copy-start | bytes 4325380
  167.4 11.4 %copy-start.21 = (bf16[1024,2048]{1,0:T(8,128)(2,1)S(1)}, bf16[1024,2048]{1,0:T(8,128)(2,1)}, u32[]{:S(2)}) copy-start(bf16[1024,2048]{1,0:T(8,128)(2,1)} %get-tuple-element.28) | copy-start | bytes 12582916
  168.9 35.3 %collective-permute-start.22 = (bf16[256,704]{0,1:T(8,128)(2,1)}, bf16[256,704]{0,1:T(8,128)(2,1)S(1)}, u32[]{:S(2)}, u32[]{:S(2)}) collective-permute-start(bf16[256,704]{0,1:T(8,128)(2,1)} %get-tuple-element.35), channel_id=1, source_target_pairs={{0,256},{64,320},{128,384},{192,448},{256,0},{320,64},{384,128},{4... | collective-permute-start | bytes 1081352 | tf_op jit(solution)/shard_map/ppermute | solution.py:22
  171.7 32.5 %collective-permute-start.23 = (bf16[256,704]{0,1:T(8,128)(2,1)}, bf16[256,704]{0,1:T(8,128)(2,1)}, u32[]{:S(2)}, u32[]{:S(2)}) collective-permute-start(bf16[256,704]{0,1:T(8,128)(2,1)} %get-tuple-element.37), channel_id=1, source_target_pairs={{0,128},{64,192},{128,256},{192,320},{256,384},{320,448},{384,0},{... | collective-permute-start | bytes 1081352 | tf_op jit(solution)/shard_map/ppermute | solution.py:22
  173.8 30.5 %collective-permute-start.24 = (bf16[256,704]{0,1:T(8,128)(2,1)}, bf16[256,704]{0,1:T(8,128)(2,1)}, u32[]{:S(2)}, u32[]{:S(2)}) collective-permute-start(bf16[256,704]{0,1:T(8,128)(2,1)} %get-tuple-element.36), channel_id=1, source_target_pairs={{0,384},{64,448},{128,0},{192,64},{256,128},{320,192},{384,256},{4... | collective-permute-start | bytes 1081352 | tf_op jit(solution)/shard_map/ppermute | solution.py:22
  (2 other events, 1.8 us)
